TPU v7x, 8 devices: a whole 2x2x1 slice. The times are simulated.
8 devices in a mesh: dp: 1 (over z), tp: 2 (over y), sp: 4 (over x, core).
Axes of the slice: x: 2, y: 2, z: 1, core: 2. Of those that a mesh axis runs over, the one named last changes fastest.
Arguments:
- tok_emb: bfloat16 [4, 32, 4096], P(None, 'dp')
- lengths: int32 [32], P('dp')
- key_cache: bfloat16 [2, 32, 1024, 8, 128], P(None, 'dp', 'sp', 'tp')
- val_cache: bfloat16 [2, 32, 1024, 8, 128], P(None, 'dp', 'sp', 'tp')
- gain_attn: bfloat16 [2, 4096], replicated
- gain_mlp: bfloat16 [2, 4096], replicated
- w_query: bfloat16 [2, 4096, 4096], P(None, None, 'tp')
- w_key: bfloat16 [2, 4096, 1024], P(None, None, 'tp')
- w_value: bfloat16 [2, 4096, 1024], P(None, None, 'tp')
- w_out: bfloat16 [2, 4096, 4096], P(None, 'tp')
- w_gate: bfloat16 [2, 4096, 14336], P(None, None, 'tp')
- w_up: bfloat16 [2, 4096, 14336], P(None, None, 'tp')
- w_down: bfloat16 [2, 14336, 4096], P(None, 'tp')
Outputs:
- output 1: bfloat16 [4, 32, 4096], P(None, 'dp')
- output 2: bfloat16 [2, 32, 1024, 8, 128], P(None, 'dp', 'sp', 'tp')
- output 3: bfloat16 [2, 32, 1024, 8, 128], P(None, 'dp', 'sp', 'tp')
All inputs are finite; a program needn't handle non-finite values.
Results may differ from a plain program's by a relative error of at most 0.0144379.
Values sent between devices are 32-bit elements.
A program may use at most 2 GiB of HBM per device.

v0:
```python
import jax
import jax.numpy as jnp
from jax import lax
from jax.sharding import PartitionSpec as P

EPS = 1e-5
ROPE_BASE = 500000.0


def rms_norm(hidden, gain_vec):
    x_float = hidden.astype(jnp.float32)
    inv_rms = lax.rsqrt(jnp.mean(x_float * x_float, axis=-1, keepdims=True) + EPS)
    return (x_float * inv_rms * gain_vec.astype(jnp.float32)).astype(jnp.bfloat16)


def rotary(in_vecs, positions):
    head_dim = in_vecs.shape[-1]
    half_dim = head_dim // 2
    inv_freq = 1.0 / (ROPE_BASE ** (jnp.arange(half_dim).astype(jnp.float32) * 2.0 / head_dim))
    angles = positions.astype(jnp.float32)[:, None] * inv_freq[None, :]
    cos_a = jnp.cos(angles)[:, None, :]
    sin_a = jnp.sin(angles)[:, None, :]
    front_half = in_vecs[..., :half_dim]
    back_half = in_vecs[..., half_dim:]
    return jnp.concatenate([front_half * cos_a - back_half * sin_a, back_half * cos_a + front_half * sin_a], axis=-1)


def project(normed, weight):
    return jnp.dot(normed, weight, preferred_element_type=jnp.float32)


def solution(mesh):
    sp_size = mesh.shape['sp']

    def local_fn(tok_emb, lengths, key_cache, val_cache, gain_attn, gain_mlp, w_query, w_key, w_value, w_out, w_gate, w_up, w_down):
        n_steps, n_batch, _ = tok_emb.shape
        n_layers, _, loc_len, kv_loc, head_dim = key_cache.shape
        heads_loc = w_query.shape[2] // head_dim
        group_size = heads_loc // kv_loc
        my_sp = lax.axis_index('sp')
        slot_pos = jnp.arange(loc_len) * sp_size + my_sp
        row_ids = jnp.arange(n_batch)
        new_keys = key_cache
        new_vals = val_cache
        hidden_list = []
        for step_idx in range(n_steps):
            cur_pos = lengths + step_idx
            write_slot = jnp.where(cur_pos % sp_size == my_sp, cur_pos // sp_size, loc_len)
            valid_mask = (slot_pos[None, :] <= cur_pos[:, None])[:, None, None, :]
            hidden = tok_emb[step_idx]
            for layer_idx in range(n_layers):
                normed = rms_norm(hidden, gain_attn[layer_idx])
                q_vec = project(normed, w_query[layer_idx]).reshape(n_batch, heads_loc, head_dim)
                k_vec = project(normed, w_key[layer_idx]).reshape(n_batch, kv_loc, head_dim)
                v_vec = project(normed, w_value[layer_idx]).reshape(n_batch, kv_loc, head_dim).astype(jnp.bfloat16)
                q_rot = rotary(q_vec, cur_pos).astype(jnp.bfloat16).reshape(n_batch, kv_loc, group_size, head_dim)
                k_rot = rotary(k_vec, cur_pos).astype(jnp.bfloat16)
                new_keys = new_keys.at[layer_idx, row_ids, write_slot].set(k_rot, mode='drop')
                new_vals = new_vals.at[layer_idx, row_ids, write_slot].set(v_vec, mode='drop')
                scores = jnp.einsum('bkgd,bjkd->bkgj', q_rot, new_keys[layer_idx], preferred_element_type=jnp.float32) * head_dim ** -0.5
                scores = jnp.where(valid_mask, scores, -1e30)
                loc_max = jnp.max(scores, axis=-1, keepdims=True)
                prob_w = jnp.exp(scores - loc_max)
                loc_sum = jnp.sum(prob_w, axis=-1, keepdims=True)
                loc_out = jnp.einsum('bkgj,bjkd->bkgd', prob_w.astype(jnp.bfloat16), new_vals[layer_idx], preferred_element_type=jnp.float32)
                glob_max = lax.pmax(loc_max, 'sp')
                rescale = jnp.exp(loc_max - glob_max)
                merged = lax.psum(jnp.concatenate([loc_out, loc_sum], axis=-1) * rescale, 'sp')
                attn_out = (merged[..., :head_dim] / merged[..., head_dim:]).astype(jnp.bfloat16).reshape(n_batch, heads_loc * head_dim)
                proj_sum = lax.psum(project(attn_out, w_out[layer_idx]), 'tp')
                hidden = (hidden.astype(jnp.float32) + proj_sum).astype(jnp.bfloat16)
                normed = rms_norm(hidden, gain_mlp[layer_idx])
                mlp_act = (jax.nn.silu(project(normed, w_gate[layer_idx])) * project(normed, w_up[layer_idx])).astype(jnp.bfloat16)
                down_sum = lax.psum(project(mlp_act, w_down[layer_idx]), 'tp')
                hidden = (hidden.astype(jnp.float32) + down_sum).astype(jnp.bfloat16)
            hidden_list.append(hidden)
        return jnp.stack(hidden_list), new_keys, new_vals

    cache_spec = P(None, 'dp', 'sp', 'tp', None)
    col_spec = P(None, None, 'tp')
    row_spec = P(None, 'tp', None)
    emb_spec = P(None, 'dp', None)
    return jax.shard_map(local_fn, mesh=mesh, in_specs=(emb_spec, P('dp'), cache_spec, cache_spec, P(), P(), col_spec, col_spec, col_spec, row_spec, col_spec, col_spec, row_spec), out_specs=(emb_spec, cache_spec, cache_spec), check_vma=False)
```

profile of v0, /device:TPU:0, one launch (start us, length us, event | category | flops | bytes accessed | tf_op | source)
XLA Modules:
  0.0 1569.5 jit_solution(13327037644563857354)
XLA Ops:
  7.2 12.1 copy.372
  90.9 23.4 %slice_bitcast_fusion = (bf16[2048,4096]{0,1:T(8,128)(2,1)}, bf16[2048,4096]{0,1:T(8,128)(2,1)}) fusion(bf16[2,4096,2048]{2,1,0:T(8,128)(2,1)} %param.19), kind=kLoop, calls=%fused_computation.104 | loop fusion | bytes 67108864 | tf_op jit(solution)/shard_map/dot_general | solution.py:29
  114.3 20.7 %copy.124 = bf16[2048,4096]{1,0:T(8,128)(2,1)} copy(bf16[2048,4096]{0,1:T(8,128)(2,1)} %get-tuple-element.51) | data formatting | bytes 33554432 | tf_op jit(solution)/shard_map/dot_general | solution.py:29
  135.0 9.1 fusion.459
  156.1 13.7 pmax.56
  187.8 8.9 fusion.474
  196.8 8.6 fusion.469
  207.7 8.7 fusion.464
  235.8 19.3 %all-reduce.22.cloned.1.call-done = f32[32,4096]{1,0:T(8,128)} async-done(((f32[32,4096]{1,0:T(8,128)}), f32[32,4096]{1,0:T(8,128)}) %all-reduce.22.cloned.1.call-update) | async-done | bytes 524304 | tf_op jit(solution)/shard_map/psum | solution.py:70
  256.3 21.6 %fusion.46 = f32[32,7168]{1,0:T(8,128)} fusion(bf16[2,4096,7168]{2,1,0:T(8,128)(2,1)} %param.23, bf16[32,4096]{1,0:T(8,128)(2,1)S(1)} %get-tuple-element.49, f32[4096]{0:T(1024)S(1)} %bitcast.626, f32[32]{0:T(128)S(1)} %add_rsqrt_fusion.14), kind=kOutput, calls=%fused_computation.62 | convolution fusion | flops 1879572480 | bytes 59916416 | tf_op jit(solution)/shard_map/dot_general | solution.py:29
  277.9 39.3 %fusion.30 = f32[32,4096]{1,0:T(8,128)} fusion(bf16[2,7168,4096]{2,1,0:T(8,128)(2,1)} %param.25, bf16[2,4096,7168]{2,1,0:T(8,128)(2,1)} %param.24, f32[32,7168]{1,0:T(8,128)} %fusion.46, bf16[32,4096]{1,0:T(8,128)(2,1)S(1)} %get-tuple-element.49, f32[4096]{0:T(1024)S(1)} %bitcast.627, f32[32]{0:T(128)S(1)} %add_rsqrt_fusion.14), kind=kOutput, calls=%fused_computation.46 | convolution fusion | flops 3759996928 | bytes 119160960 | tf_op jit(solution)/shard_map/dot_general | solution.py:29
  331.9 20.8 %copy.137 = bf16[2048,4096]{1,0:T(8,128)(2,1)} copy(bf16[2048,4096]{0,1:T(8,128)(2,1)} %get-tuple-element.50) | data formatting | bytes 33554432 | tf_op jit(solution)/shard_map/dot_general | solution.py:29
  374.0 8.6 fusion.439
  403.9 12.0 pmax.58
  439.0 26.7 %all-reduce.26.cloned.1.call-done = f32[32,4,4,129]{3,2,1,0:T(4,128)} async-done(((f32[32,4,4,129]{3,2,1,0:T(4,128)}), f32[32,4,4,129]{3,2,1,0:T(4,128)}) %all-reduce.26.cloned.1.call-update) | async-done | bytes 264208 | tf_op jit(solution)/shard_map/psum | solution.py:68
  484.8 15.1 all-reduce.28.cloned.1.call-done
  501.1 21.7 %fusion.44 = f32[32,7168]{1,0:T(8,128)} fusion(bf16[2,4096,7168]{2,1,0:T(8,128)(2,1)} %param.23, bf16[32,4096]{1,0:T(8,128)(2,1)S(1)} %get-tuple-element.45, f32[32]{0:T(128)S(1)} %add_rsqrt_fusion.10, f32[4096]{0:T(1024)S(1)} %bitcast.628), kind=kOutput, calls=%fused_computation.60 | convolution fusion | flops 1879572480 | bytes 59916416 | tf_op jit(solution)/shard_map/dot_general | solution.py:29
  522.9 39.4 %fusion.28 = f32[32,4096]{1,0:T(8,128)} fusion(bf16[2,7168,4096]{2,1,0:T(8,128)(2,1)} %param.25, bf16[2,4096,7168]{2,1,0:T(8,128)(2,1)} %param.24, f32[32,7168]{1,0:T(8,128)} %fusion.44, bf16[32,4096]{1,0:T(8,128)(2,1)S(1)} %get-tuple-element.45, f32[32]{0:T(128)S(1)} %add_rsqrt_fusion.10, f32[4096]{0:T(1024)S(1)} %bitcast.629), kind=kOutput, calls=%fused_computation.44 | convolution fusion | flops 3759996928 | bytes 119160960 | tf_op jit(solution)/shard_map/dot_general | solution.py:29
  567.8 17.5 %all-reduce.30.cloned.1.call-done = f32[32,4096]{1,0:T(8,128)} async-done(((f32[32,4096]{1,0:T(8,128)}), f32[32,4096]{1,0:T(8,128)}) %all-reduce.30.cloned.1.call-update) | async-done | bytes 524304 | tf_op jit(solution)/shard_map/psum | solution.py:74
  593.8 8.8 fusion.444
  634.8 11.0 pmax.60
  668.9 27.2 %all-reduce.32.cloned.1.call-done = f32[32,4,4,129]{3,2,1,0:T(4,128)} async-done(((f32[32,4,4,129]{3,2,1,0:T(4,128)}), f32[32,4,4,129]{3,2,1,0:T(4,128)}) %all-reduce.32.cloned.1.call-update) | async-done | bytes 264208 | tf_op jit(solution)/shard_map/psum | solution.py:68
  715.3 15.1 all-reduce.34.cloned.1.call-done
  731.6 20.7 %fusion.42 = f32[32,7168]{1,0:T(8,128)S(1)} fusion(bf16[2,4096,7168]{2,1,0:T(8,128)(2,1)} %param.23, bf16[32,4096]{1,0:T(8,128)(2,1)S(1)} %get-tuple-element.41, f32[32]{0:T(128)S(1)} %add_rsqrt_fusion.6, f32[4096]{0:T(1024)S(1)} %bitcast.630), kind=kOutput, calls=%fused_computation.58 | convolution fusion | flops 1879572480 | bytes 59916416 | tf_op jit(solution)/shard_map/dot_general | solution.py:29
  752.3 39.1 %fusion.26 = f32[32,4096]{1,0:T(8,128)} fusion(bf16[2,7168,4096]{2,1,0:T(8,128)(2,1)} %param.25, bf16[2,4096,7168]{2,1,0:T(8,128)(2,1)} %param.24, f32[32,7168]{1,0:T(8,128)S(1)} %fusion.42, bf16[32,4096]{1,0:T(8,128)(2,1)S(1)} %get-tuple-element.41, f32[32]{0:T(128)S(1)} %add_rsqrt_fusion.6, f32[4096]{0:T(1024)S(1)} %bitcast.631), kind=kOutput, calls=%fused_computation.42 | convolution fusion | flops 3759996928 | bytes 119160960 | tf_op jit(solution)/shard_map/dot_general | solution.py:29
  797.1 17.3 %all-reduce.36.cloned.1.call-done = f32[32,4096]{1,0:T(8,128)} async-done(((f32[32,4096]{1,0:T(8,128)}), f32[32,4096]{1,0:T(8,128)}) %all-reduce.36.cloned.1.call-update) | async-done | bytes 524304 | tf_op jit(solution)/shard_map/psum | solution.py:74
  822.8 8.6 fusion.449
  863.4 11.7 pmax.62
  898.0 27.1 %all-reduce.38.cloned.1.call-done = f32[32,4,4,129]{3,2,1,0:T(4,128)} async-done(((f32[32,4,4,129]{3,2,1,0:T(4,128)}), f32[32,4,4,129]{3,2,1,0:T(4,128)}) %all-reduce.38.cloned.1.call-update) | async-done | bytes 264208 | tf_op jit(solution)/shard_map/psum | solution.py:68
  944.3 15.1 all-reduce.40.cloned.1.call-done
  960.6 20.7 %fusion.40 = f32[32,7168]{1,0:T(8,128)S(1)} fusion(bf16[2,4096,7168]{2,1,0:T(8,128)(2,1)} %param.23, bf16[32,4096]{1,0:T(8,128)(2,1)S(1)} %get-tuple-element.37, f32[32]{0:T(128)S(1)} %add_rsqrt_fusion.2, f32[4096]{0:T(1024)S(1)} %bitcast.632), kind=kOutput, calls=%fused_computation.56 | convolution fusion | flops 1879572480 | bytes 59916416 | tf_op jit(solution)/shard_map/dot_general | solution.py:29
  981.3 39.1 %fusion.24 = f32[32,4096]{1,0:T(8,128)} fusion(bf16[2,7168,4096]{2,1,0:T(8,128)(2,1)} %param.25, bf16[2,4096,7168]{2,1,0:T(8,128)(2,1)} %param.24, f32[32,7168]{1,0:T(8,128)S(1)} %fusion.40, bf16[32,4096]{1,0:T(8,128)(2,1)S(1)} %get-tuple-element.37, f32[32]{0:T(128)S(1)} %add_rsqrt_fusion.2, f32[4096]{0:T(1024)S(1)} %bitcast.633), kind=kOutput, calls=%fused_computation.40 | convolution fusion | flops 3759996928 | bytes 119160960 | tf_op jit(solution)/shard_map/dot_general | solution.py:29
  1026.3 17.2 %all-reduce.42.cloned.1.call-done = f32[32,4096]{1,0:T(8,128)} async-done(((f32[32,4096]{1,0:T(8,128)}), f32[32,4096]{1,0:T(8,128)}) %all-reduce.42.cloned.1.call-update) | async-done | bytes 524304 | tf_op jit(solution)/shard_map/psum | solution.py:74
  1044.9 8.6 fusion.454
  1081.0 14.1 all-reduce.1
  1106.1 45.5 %all-reduce.44.cloned.1.call-done = (f32[32,4,4,129]{3,2,1,0:T(4,128)}, f32[32,4,4,129]{3,2,1,0:T(4,128)}, f32[32,4,4,129]{3,2,1,0:T(4,128)}, f32[32,4,4,129]{3,2,1,0:T(4,128)}) async-done(((f32[32,4,4,129]{3,2,1,0:T(4,128)}, f32[32,4,4,129]{3,2,1,0:T(4,128)}, f32[32,4,4,129]{3,2,1,0:T(4,128)}, f32[32,4,4,129]{3,2,1,0:T(4,128)}), (f32[32,4,4,129]{3,2,1,0:T(4,128)}, f32[32,4,4,129]{3,2,1,0:T(4,128)}, ...) | async-done | bytes 1056784 | tf_op jit(solution)/shard_map/psum | solution.py:68
  1172.1 8.1 fusion.76
  1180.2 8.2 fusion.74
  1196.8 57.2 %all-reduce.48.cloned.1.call-done = (f32[32,4096]{1,0:T(8,128)}, f32[32,4096]{1,0:T(8,128)}, f32[32,4096]{1,0:T(8,128)}, f32[32,4096]{1,0:T(8,128)}) async-done(((f32[32,4096]{1,0:T(8,128)}, f32[32,4096]{1,0:T(8,128)}, f32[32,4096]{1,0:T(8,128)}, f32[32,4096]{1,0:T(8,128)}), (f32[32,4096]{1,0:T(8,128)}, f32[32,4096]{1,0:T(8,128)}, f32[32,4096]{1,0:T(8,128)}, ...) | async-done | bytes 2097168 | tf_op jit(solution)/shard_map/psum | solution.py:70
  1260.2 20.8 %fusion.22 = f32[32,7168]{1,0:T(8,128)S(1)} fusion(bf16[2,4096,7168]{2,1,0:T(8,128)(2,1)} %param.23, bf16[32,4096]{1,0:T(8,128)(2,1)S(1)} %get-tuple-element.27, f32[4096]{0:T(1024)S(1)} %bitcast.618, f32[32]{0:T(128)S(1)} %add_rsqrt_fusion.12), kind=kOutput, calls=%fused_computation.38 | convolution fusion | flops 1879572480 | bytes 59916416 | tf_op jit(solution)/shard_map/dot_general | solution.py:29
  1281.0 39.1 %fusion.6 = f32[32,4096]{1,0:T(8,128)} fusion(bf16[2,7168,4096]{2,1,0:T(8,128)(2,1)} %param.25, bf16[2,4096,7168]{2,1,0:T(8,128)(2,1)} %param.24, f32[32,7168]{1,0:T(8,128)S(1)} %fusion.22, bf16[32,4096]{1,0:T(8,128)(2,1)S(1)} %get-tuple-element.27, f32[4096]{0:T(1024)S(1)} %bitcast.619, f32[32]{0:T(128)S(1)} %add_rsqrt_fusion.12), kind=kOutput, calls=%fused_computation.22 | convolution fusion | flops 3759996928 | bytes 119160960 | tf_op jit(solution)/shard_map/dot_general | solution.py:29
  1320.1 20.7 %fusion.20 = f32[32,7168]{1,0:T(8,128)S(1)} fusion(bf16[2,4096,7168]{2,1,0:T(8,128)(2,1)} %param.23, bf16[32,4096]{1,0:T(8,128)(2,1)S(1)} %get-tuple-element.29, f32[32]{0:T(128)S(1)} %add_rsqrt_fusion.8, f32[4096]{0:T(1024)S(1)} %bitcast.620), kind=kOutput, calls=%fused_computation.36 | convolution fusion | flops 1879572480 | bytes 59916416 | tf_op jit(solution)/shard_map/dot_general | solution.py:29
  1340.8 39.1 %fusion.4 = f32[32,4096]{1,0:T(8,128)} fusion(bf16[2,7168,4096]{2,1,0:T(8,128)(2,1)} %param.25, bf16[2,4096,7168]{2,1,0:T(8,128)(2,1)} %param.24, f32[32,7168]{1,0:T(8,128)S(1)} %fusion.20, bf16[32,4096]{1,0:T(8,128)(2,1)S(1)} %get-tuple-element.29, f32[32]{0:T(128)S(1)} %add_rsqrt_fusion.8, f32[4096]{0:T(1024)S(1)} %bitcast.621), kind=kOutput, calls=%fused_computation.20 | convolution fusion | flops 3759996928 | bytes 119160960 | tf_op jit(solution)/shard_map/dot_general | solution.py:29
  1379.9 20.7 %fusion.18 = f32[32,7168]{1,0:T(8,128)S(1)} fusion(bf16[2,4096,7168]{2,1,0:T(8,128)(2,1)} %param.23, bf16[32,4096]{1,0:T(8,128)(2,1)S(1)} %get-tuple-element.31, f32[32]{0:T(128)S(1)} %add_rsqrt_fusion.4, f32[4096]{0:T(1024)S(1)} %bitcast.622), kind=kOutput, calls=%fused_computation.34 | convolution fusion | flops 1879572480 | bytes 59916416 | tf_op jit(solution)/shard_map/dot_general | solution.py:29
  1400.6 39.4 %fusion.2 = f32[32,4096]{1,0:T(8,128)} fusion(bf16[2,7168,4096]{2,1,0:T(8,128)(2,1)} %param.25, bf16[2,4096,7168]{2,1,0:T(8,128)(2,1)} %param.24, f32[32,7168]{1,0:T(8,128)S(1)} %fusion.18, bf16[32,4096]{1,0:T(8,128)(2,1)S(1)} %get-tuple-element.31, f32[32]{0:T(128)S(1)} %add_rsqrt_fusion.4, f32[4096]{0:T(1024)S(1)} %bitcast.623), kind=kOutput, calls=%fused_computation.18 | convolution fusion | flops 3759996928 | bytes 119160960 | tf_op jit(solution)/shard_map/dot_general | solution.py:29
  1440.0 20.7 %fusion.16 = f32[32,7168]{1,0:T(8,128)S(1)} fusion(bf16[2,4096,7168]{2,1,0:T(8,128)(2,1)} %param.23, bf16[32,4096]{1,0:T(8,128)(2,1)S(1)} %copy-done.20, f32[32]{0:T(128)S(1)} %copy-done.57, f32[4096]{0:T(1024)S(1)} %bitcast.624), kind=kOutput, calls=%fused_computation.32 | convolution fusion | flops 1879572480 | bytes 59916416 | tf_op jit(solution)/shard_map/dot_general | solution.py:29
  1460.6 39.1 %fusion = f32[32,4096]{1,0:T(8,128)} fusion(bf16[2,7168,4096]{2,1,0:T(8,128)(2,1)} %param.25, bf16[2,4096,7168]{2,1,0:T(8,128)(2,1)} %param.24, f32[32,7168]{1,0:T(8,128)S(1)} %fusion.16, bf16[32,4096]{1,0:T(8,128)(2,1)S(1)} %copy-done.20, f32[32]{0:T(128)S(1)} %copy-done.57, f32[4096]{0:T(1024)S(1)} %bitcast.625), kind=kOutput, calls=%fused_computation.16 | convolution fusion | flops 3759996928 | bytes 119160960 | tf_op jit(solution)/shard_map/dot_general | solution.py:29
  1499.8 57.3 %all-reduce.46.cloned.1.call-done = (f32[32,4096]{1,0:T(8,128)}, f32[32,4096]{1,0:T(8,128)}, f32[32,4096]{1,0:T(8,128)}, f32[32,4096]{1,0:T(8,128)}) async-done(((f32[32,4096]{1,0:T(8,128)}, f32[32,4096]{1,0:T(8,128)}, f32[32,4096]{1,0:T(8,128)}, f32[32,4096]{1,0:T(8,128)}), (f32[32,4096]{1,0:T(8,128)}, f32[32,4096]{1,0:T(8,128)}, f32[32,4096]{1,0:T(8,128)}, ...) | async-done | bytes 2097168 | tf_op jit(solution)/shard_map/psum | solution.py:74
  (385 shorter events, 489.2 us)
Async XLA Ops:
  7.2 213.6 %all-reduce.20.cloned.1.call-start = ((), (), s32[]{:S(2)}) async-start(), calls=%async_computation | async-start | bytes 1048576 | tf_op jit(solution)/shard_map/psum | solution.py:68
  48.2 95.9 %copy-start.33 = (f32[32,64]{1,0:T(8,128)}, f32[32,64]{1,0:T(8,128)S(1)}, u32[]{:S(2)}) copy-start(f32[32,64]{1,0:T(8,128)S(1)} %get-tuple-element.123) | copy-start | bytes 24580
  48.2 95.9 %copy-start.35 = (f32[32,64]{1,0:T(8,128)}, f32[32,64]{1,0:T(8,128)S(1)}, u32[]{:S(2)}) copy-start(f32[32,64]{1,0:T(8,128)S(1)} %get-tuple-element.124) | copy-start | bytes 24580
  171.7 83.4 %all-reduce.22.cloned.1.call-start = ((), (), s32[]{:S(2)}) async-start(), calls=%async_computation.1 | async-start | bytes 1048576 | tf_op jit(solution)/shard_map/psum | solution.py:70
  207.7 24.4 %copy-start.31 = (f32[32,64]{1,0:T(8,128)S(1)}, f32[32,64]{1,0:T(8,128)}, u32[]{:S(2)}) copy-start(f32[32,64]{1,0:T(8,128)} %get-tuple-element.119) | copy-start | bytes 24580
  207.7 24.4 %copy-start.32 = (f32[32,64]{1,0:T(8,128)S(1)}, f32[32,64]{1,0:T(8,128)}, u32[]{:S(2)}) copy-start(f32[32,64]{1,0:T(8,128)} %get-tuple-element.120) | copy-start | bytes 24580
  207.7 24.5 %copy-start.3 = (bf16[4,32,4096]{2,1,0:T(8,128)(2,1)S(1)}, bf16[4,32,4096]{2,1,0:T(8,128)(2,1)}, u32[]{:S(2)}) copy-start(bf16[4,32,4096]{2,1,0:T(8,128)(2,1)} %param.13) | copy-start | bytes 3145732
  217.9 60.1 %copy-start.48 = (f32[1,4096]{1,0:T(1,128)}, f32[1,4096]{1,0:T(1,128)S(1)}, u32[]{:S(2)}) copy-start(f32[1,4096]{1,0:T(1,128)S(1)} %get-tuple-element.89) | copy-start | bytes 49156
  232.1 122.7 %all-reduce.24.cloned.1.call-start = ((), (), s32[]{:S(2)}) async-start(), calls=%async_computation.2 | async-start | bytes 1048576 | tf_op jit(solution)/shard_map/psum | solution.py:74
  317.3 148.4 %all-reduce.26.cloned.1.call-start = ((), (), s32[]{:S(2)}) async-start(), calls=%async_computation.3 | async-start | bytes 1048576 | tf_op jit(solution)/shard_map/psum | solution.py:68
  331.9 31.3 %copy-start.34 = (f32[32,64]{1,0:T(8,128)S(1)}, f32[32,64]{1,0:T(8,128)}, u32[]{:S(2)}) copy-start(f32[32,64]{1,0:T(8,128)} %copy-done.33) | copy-start | bytes 24580
  331.9 31.3 %copy-start.36 = (f32[32,64]{1,0:T(8,128)S(1)}, f32[32,64]{1,0:T(8,128)}, u32[]{:S(2)}) copy-start(f32[32,64]{1,0:T(8,128)} %copy-done.35) | copy-start | bytes 24580
  331.9 31.5 %copy-start.16 = (s32[32]{0:T(128)S(1)}, s32[32]{0:T(128)}, u32[]{:S(2)}) copy-start(s32[32]{0:T(128)} %get-tuple-element.118) | copy-start | bytes 388
  355.9 34.7 %copy-start.5 = (bf16[32,4096]{1,0:T(8,128)(2,1)}, bf16[32,4096]{1,0:T(8,128)(2,1)S(1)}, u32[]{:S(2)}) copy-start(bf16[32,4096]{1,0:T(8,128)(2,1)S(1)} %get-tuple-element.47) | copy-start | bytes 786436
  436.2 40.7 %copy-start.54 = (pred[32,256]{1,0:T(8,128)(4,1)S(1)}, pred[32,256]{1,0:T(8,128)(4,1)}, u32[]{:S(2)}) copy-start(pred[32,256]{1,0:T(8,128)(4,1)} %copy-done.53) | copy-start | bytes 24580
  438.6 62.5 %copy-start.49 = (f32[1,4096]{1,0:T(1,128)S(1)}, f32[1,4096]{1,0:T(1,128)}, u32[]{:S(2)}) copy-start(f32[1,4096]{1,0:T(1,128)} %copy-done.48) | copy-start | bytes 49156
  438.6 61.3 %all-reduce.28.cloned.1.call-start = ((), (), s32[]{:S(2)}) async-start(), calls=%async_computation.4 | async-start | bytes 1048576 | tf_op jit(solution)/shard_map/psum | solution.py:70
  476.9 108.4 %all-reduce.30.cloned.1.call-start = ((), (), s32[]{:S(2)}) async-start(), calls=%async_computation.5 | async-start | bytes 1048576 | tf_op jit(solution)/shard_map/psum | solution.py:74
  482.8 79.6 %copy-start.23 = (f32[32,4,4]{2,1,0:T(4,128)}, f32[32,4,4]{2,1,0:T(4,128)S(1)}, u32[]{:S(2)}) copy-start(f32[32,4,4]{2,1,0:T(4,128)S(1)} %get-tuple-element.139) | copy-start | bytes 6148
  562.3 40.5 %copy-start.14 = (s32[32]{0:T(128)S(1)}, s32[32]{0:T(128)}, u32[]{:S(2)}) copy-start(s32[32]{0:T(128)} %get-tuple-element.116) | copy-start | bytes 388
  562.3 133.8 %all-reduce.32.cloned.1.call-start = ((), (), s32[]{:S(2)}) async-start(), calls=%async_computation.6 | async-start | bytes 1048576 | tf_op jit(solution)/shard_map/psum | solution.py:68
  593.7 28.1 %copy-start.13 = (s32[32]{0:T(128)S(1)}, s32[32]{0:T(128)}, u32[]{:S(2)}) copy-start(s32[32]{0:T(128)} %get-tuple-element.114) | copy-start | bytes 388
  668.2 62.2 %all-reduce.34.cloned.1.call-start = ((), (), s32[]{:S(2)}) async-start(), calls=%async_computation.7 | async-start | bytes 1048576 | tf_op jit(solution)/shard_map/psum | solution.py:70
  707.4 107.1 %all-reduce.36.cloned.1.call-start = ((), (), s32[]{:S(2)}) async-start(), calls=%async_computation.8 | async-start | bytes 1048576 | tf_op jit(solution)/shard_map/psum | solution.py:74
  791.4 40.0 %copy-start.28 = (f32[32,64]{1,0:T(8,128)S(1)}, f32[32,64]{1,0:T(8,128)}, u32[]{:S(2)}) copy-start(f32[32,64]{1,0:T(8,128)} %get-tuple-element.121) | copy-start | bytes 24580
  791.5 40.0 %copy-start.30 = (f32[32,64]{1,0:T(8,128)S(1)}, f32[32,64]{1,0:T(8,128)}, u32[]{:S(2)}) copy-start(f32[32,64]{1,0:T(8,128)} %get-tuple-element.122) | copy-start | bytes 24580
  791.5 40.2 %copy-start.12 = (s32[32]{0:T(128)S(1)}, s32[32]{0:T(128)}, u32[]{:S(2)}) copy-start(s32[32]{0:T(128)} %get-tuple-element.117) | copy-start | bytes 388
  791.5 133.7 %all-reduce.38.cloned.1.call-start = ((), (), s32[]{:S(2)}) async-start(), calls=%async_computation.9 | async-start | bytes 1048576 | tf_op jit(solution)/shard_map/psum | solution.py:68
  822.8 27.4 %copy-start.11 = (s32[32]{0:T(128)S(1)}, s32[32]{0:T(128)}, u32[]{:S(2)}) copy-start(s32[32]{0:T(128)} %get-tuple-element.115) | copy-start | bytes 388
  822.8 27.4 %copy-start.43 = (bf16[32,4,128]{2,1,0:T(4,128)(2,1)S(1)}, bf16[32,4,128]{2,1,0:T(4,128)(2,1)}, u32[]{:S(2)}) copy-start(bf16[32,4,128]{2,1,0:T(4,128)(2,1)} %copy.192) | copy-start | bytes 98308
  895.3 41.2 %copy-start.52 = (pred[32,256]{1,0:T(8,128)(4,1)S(1)}, pred[32,256]{1,0:T(8,128)(4,1)}, u32[]{:S(2)}) copy-start(pred[32,256]{1,0:T(8,128)(4,1)} %get-tuple-element.94) | copy-start | bytes 24580
  897.7 61.7 %all-reduce.40.cloned.1.call-start = ((), (), s32[]{:S(2)}) async-start(), calls=%async_computation.10 | async-start | bytes 1048576 | tf_op jit(solution)/shard_map/psum | solution.py:70
  936.4 107.1 %all-reduce.42.cloned.1.call-start = ((), (), s32[]{:S(2)}) async-start(), calls=%async_computation.11 | async-start | bytes 1048576 | tf_op jit(solution)/shard_map/psum | solution.py:74
  942.3 78.7 %copy-start.25 = (f32[32,4,4]{2,1,0:T(4,128)}, f32[32,4,4]{2,1,0:T(4,128)S(1)}, u32[]{:S(2)}) copy-start(f32[32,4,4]{2,1,0:T(4,128)S(1)} %get-tuple-element.135) | copy-start | bytes 6148
  1020.5 131.1 %all-reduce.44.cloned.1.call-start = ((), (), s32[]{:S(2)}) async-start(), calls=%async_computation.12 | async-start | bytes 4194304 | tf_op jit(solution)/shard_map/psum | solution.py:68
  1026.3 34.9 %copy-start.10 = (s32[32]{0:T(128)S(1)}, s32[32]{0:T(128)}, u32[]{:S(2)}) copy-start(s32[32]{0:T(128)} %get-tuple-element.111) | copy-start | bytes 388
  1077.2 24.8 %copy-start.17 = (f32[32,4,4,1]{3,2,1,0:T(4,128)S(1)}, f32[32,4,4,1]{3,2,1,0:T(4,128)}, u32[]{:S(2)}) copy-start(f32[32,4,4,1]{3,2,1,0:T(4,128)} %copy.147) | copy-start | bytes 6148
  1077.2 24.8 %copy-start.37 = (f32[32,4,4,128]{3,2,1,0:T(4,128)S(1)}, f32[32,4,4,128]{3,2,1,0:T(4,128)}, u32[]{:S(2)}) copy-start(f32[32,4,4,128]{3,2,1,0:T(4,128)} %fusion.108) | copy-start | bytes 786436
  1079.7 24.4 %copy-start.19 = (f32[32,4,4,1]{3,2,1,0:T(4,128)S(1)}, f32[32,4,4,1]{3,2,1,0:T(4,128)}, u32[]{:S(2)}) copy-start(f32[32,4,4,1]{3,2,1,0:T(4,128)} %copy.187) | copy-start | bytes 6148
  1079.7 24.4 %copy-start.39 = (f32[32,4,4,128]{3,2,1,0:T(4,128)S(1)}, f32[32,4,4,128]{3,2,1,0:T(4,128)}, u32[]{:S(2)}) copy-start(f32[32,4,4,128]{3,2,1,0:T(4,128)} %fusion.100) | copy-start | bytes 786436
  1106.1 147.9 %all-reduce.48.cloned.1.call-start = ((), (), s32[]{:S(2)}) async-start(), calls=%async_computation.14 | async-start | bytes 4194304 | tf_op jit(solution)/shard_map/psum | solution.py:70
  1180.2 77.5 %copy-start.8 = (bf16[32,4096]{1,0:T(8,128)(2,1)S(1)}, bf16[32,4096]{1,0:T(8,128)(2,1)}, u32[]{:S(2)}) copy-start(bf16[32,4096]{1,0:T(8,128)(2,1)} %copy-done.7) | copy-start | bytes 786436
  1180.2 78.7 %copy-start.6 = (bf16[32,4096]{1,0:T(8,128)(2,1)S(1)}, bf16[32,4096]{1,0:T(8,128)(2,1)}, u32[]{:S(2)}) copy-start(bf16[32,4096]{1,0:T(8,128)(2,1)} %copy-done.5) | copy-start | bytes 786436
  1180.2 80.0 %copy-start.47 = (f32[1,4096]{1,0:T(1,128)S(1)}, f32[1,4096]{1,0:T(1,128)}, u32[]{:S(2)}) copy-start(f32[1,4096]{1,0:T(1,128)} %get-tuple-element.88) | copy-start | bytes 49156
  1196.5 360.6 %all-reduce.46.cloned.1.call-start = ((), (), s32[]{:S(2)}) async-start(), calls=%async_computation.13 | async-start | bytes 4194304 | tf_op jit(solution)/shard_map/psum | solution.py:74
  1400.6 39.4 %copy-start.20 = (bf16[32,4096]{1,0:T(8,128)(2,1)S(1)}, bf16[32,4096]{1,0:T(8,128)(2,1)}, u32[]{:S(2)}) copy-start(bf16[32,4096]{1,0:T(8,128)(2,1)} %get-tuple-element.33) | copy-start | bytes 786436
  1400.6 39.4 %copy-start.57 = (f32[32]{0:T(128)S(1)}, f32[32]{0:T(128)}, u32[]{:S(2)}) copy-start(f32[32]{0:T(128)} %add_rsqrt_fusion) | copy-start | bytes 388
  1460.6 96.5 %copy-start.22 = (bf16[32,4096]{1,0:T(8,128)(2,1)S(1)}, bf16[32,4096]{1,0:T(8,128)(2,1)}, u32[]{:S(2)}) copy-start(bf16[32,4096]{1,0:T(8,128)(2,1)} %copy-done.21) | copy-start | bytes 786436
  (25 other events, 415.6 us)
Sparse Core Ops, SparseCore 0:
  171.9 27.7 all-reduce.19
  232.2 22.8 all-reduce.21
  317.4 22.8 all-reduce.23
  438.7 26.8 all-reduce.25
  477.0 22.8 all-reduce.27
  562.4 22.8 all-reduce.29
  668.3 27.7 all-reduce.31
  707.5 22.8 all-reduce.33
  791.6 22.8 all-reduce.35
  897.8 27.3 all-reduce.37
  936.5 22.8 all-reduce.39
  1020.6 22.8 all-reduce.41
  1106.2 45.3 all-reduce.43
  1196.6 57.2 all-reduce.47
  1499.9 57.1 all-reduce.45
where the time goes:
time: 1580 us; the launch traced here: 1570 us
  matrix products  731 us (46%)
  waiting for transfers between devices  358 us (23%)
  local copies, waits for them, and re-layouts  346 us (22%)
  blocking collectives  62.6 us (4%)
  other arithmetic  54.1 us (3%)
    dot_general x48, matrix products, project(): return jnp.dot(normed, weight, preferred_element_type=jnp.float32)  672 us
    psum x5, waiting for transfers between devices, local_fn(): lax.psum(jnp.concatenate([loc_out, loc_sum], axis=-1) * rescale, 'sp')  127 us
    psum x5, waiting for transfers between devices, local_fn(): proj_sum = lax.psum(project(attn_out, w_out[layer_idx]), 'tp')  122 us
    psum x5, waiting for transfers between devices, local_fn(): down_sum = lax.psum(project(mlp_act, w_down[layer_idx]), 'tp')  109 us
    dot_general x9, local copies, waits for them, and re-layouts, project(): return jnp.dot(normed, weight, preferred_element_type=jnp.float32)  102 us
    pmax x5, blocking collectives, local_fn(): glob_max = lax.pmax(loc_max, 'sp')  62.6 us
    slice x8, local copies, waits for them, and re-layouts, local_fn(): new_keys[layer_idx]  53.8 us
    slice x8, local copies, waits for them, and re-layouts, local_fn(): new_vals[layer_idx]  53.7 us
  transfers between devices with their start and end apart: 15, of which 13 were waited for; matrix products, arithmetic and copies ran while one was open for 8% of the time, Pallas kernels for 0%

commit v1 on v0

v1 whole, which is shorter than its diff:
```python
import jax
import jax.numpy as jnp
from jax import lax
from jax.sharding import PartitionSpec as P

EPS = 1e-5
ROPE_BASE = 500000.0


def rms_norm(hidden, gain_vec):
    x_float = hidden.astype(jnp.float32)
    inv_rms = lax.rsqrt(jnp.mean(x_float * x_float, axis=-1, keepdims=True) + EPS)
    return (x_float * inv_rms * gain_vec.astype(jnp.float32)).astype(jnp.bfloat16)


def rope_tables(positions, head_dim):
    half_dim = head_dim // 2
    inv_freq = 1.0 / (ROPE_BASE ** (jnp.arange(half_dim).astype(jnp.float32) * 2.0 / head_dim))
    angles = positions.astype(jnp.float32)[:, None] * inv_freq[None, :]
    return jnp.cos(angles)[:, None, :], jnp.sin(angles)[:, None, :]


def rotary(in_vecs, cos_a, sin_a):
    half_dim = in_vecs.shape[-1] // 2
    front = in_vecs[..., :half_dim]
    back = in_vecs[..., half_dim:]
    return jnp.concatenate([front * cos_a - back * sin_a, back * cos_a + front * sin_a], axis=-1)


def project(normed, weight):
    return jnp.dot(normed, weight, preferred_element_type=jnp.float32)


def solution(mesh):
    sp_size = mesh.shape['sp']

    def local_fn(tok_emb, lengths, key_cache, val_cache, gain_attn, gain_mlp, w_query, w_key, w_value, w_out, w_gate, w_up, w_down):
        n_steps, n_batch, d_model = tok_emb.shape
        n_layers, _, loc_len, kv_loc, head_dim = key_cache.shape
        heads_loc = w_query.shape[2] // head_dim
        group = heads_loc // kv_loc
        rows = n_steps * n_batch
        my_sp = lax.axis_index('sp')
        slot_pos = jnp.arange(loc_len) * sp_size + my_sp
        row_ids = jnp.arange(n_batch)
        cur_pos = lengths[None, :] + jnp.arange(n_steps)[:, None]
        write_slot = jnp.where(cur_pos % sp_size == my_sp, cur_pos // sp_size, loc_len)
        valid = (slot_pos[None, None, :] <= cur_pos[:, :, None])
        valid = valid.transpose(1, 0, 2)[:, None, :, None, :]
        cos_a, sin_a = rope_tables(cur_pos.reshape(rows), head_dim)
        hidden = tok_emb.reshape(rows, d_model)
        new_keys, new_vals = key_cache, val_cache
        for layer in range(n_layers):
            normed = rms_norm(hidden, gain_attn[layer])
            q_vec = project(normed, w_query[layer]).reshape(rows, heads_loc, head_dim)
            k_vec = project(normed, w_key[layer]).reshape(rows, kv_loc, head_dim)
            v_vec = project(normed, w_value[layer]).reshape(n_steps, n_batch, kv_loc, head_dim).astype(jnp.bfloat16)
            q_rot = rotary(q_vec, cos_a, sin_a).astype(jnp.bfloat16).reshape(n_steps, n_batch, kv_loc, group, head_dim)
            k_rot = rotary(k_vec, cos_a, sin_a).astype(jnp.bfloat16).reshape(n_steps, n_batch, kv_loc, head_dim)
            for s in range(n_steps):
                new_keys = new_keys.at[layer, row_ids, write_slot[s]].set(k_rot[s], mode='drop')
                new_vals = new_vals.at[layer, row_ids, write_slot[s]].set(v_vec[s], mode='drop')
            scores = jnp.einsum('sbkgd,bjkd->bksgj', q_rot, new_keys[layer], preferred_element_type=jnp.float32) * head_dim ** -0.5
            scores = jnp.where(valid, scores, -1e30)
            loc_max = jnp.max(scores, axis=-1, keepdims=True)
            prob_w = jnp.exp(scores - loc_max)
            loc_sum = jnp.sum(prob_w, axis=-1, keepdims=True)
            loc_out = jnp.einsum('bksgj,bjkd->bksgd', prob_w.astype(jnp.bfloat16), new_vals[layer], preferred_element_type=jnp.float32)
            glob_max = lax.pmax(loc_max, 'sp')
            merged = lax.psum(jnp.concatenate([loc_out, loc_sum], axis=-1) * jnp.exp(loc_max - glob_max), 'sp')
            attn_out = (merged[..., :head_dim] / merged[..., head_dim:]).astype(jnp.bfloat16)
            attn_out = attn_out.transpose(2, 0, 1, 3, 4).reshape(rows, heads_loc * head_dim)
            proj_sum = lax.psum(project(attn_out, w_out[layer]), 'tp')
            hidden = (hidden.astype(jnp.float32) + proj_sum).astype(jnp.bfloat16)
            normed = rms_norm(hidden, gain_mlp[layer])
            mlp_act = (jax.nn.silu(project(normed, w_gate[layer])) * project(normed, w_up[layer])).astype(jnp.bfloat16)
            down_sum = lax.psum(project(mlp_act, w_down[layer]), 'tp')
            hidden = (hidden.astype(jnp.float32) + down_sum).astype(jnp.bfloat16)
        return hidden.reshape(n_steps, n_batch, d_model), new_keys, new_vals

    cache_spec = P(None, 'dp', 'sp', 'tp', None)
    col_spec = P(None, None, 'tp')
    row_spec = P(None, 'tp', None)
    emb_spec = P(None, 'dp', None)
    return jax.shard_map(local_fn, mesh=mesh, in_specs=(emb_spec, P('dp'), cache_spec, cache_spec, P(), P(), col_spec, col_spec, col_spec, row_spec, col_spec, col_spec, row_spec), out_specs=(emb_spec, cache_spec, cache_spec), check_vma=False)
```

time: 1580 us -> 815 us (0.52)
  matrix products: 731 us -> 191 us
  local copies, waits for them, and re-layouts: 346 us -> 250 us
  waiting for transfers between devices: 358 us -> 286 us
  blocking collectives: 62.6 us -> 30.9 us
  other arithmetic: 54.1 us -> 29.3 us
    dot_general x48 -> x12, matrix products: 672 us -> 171 us  [project(): return jnp.dot(normed, weight, preferred_element_type=jnp.float32)]
    slice x16 -> x12, local copies, waits for them, and re-layouts: 107 us -> 27.9 us  [the longest x2 16.1 us: local_fn(): new_keys[layer]]
    psum x15 -> x6, waiting for transfers between devices: 358 us -> 286 us  [the longest x2 114 us: local_fn(): proj_sum = lax.psum(project(attn_out, w_out[layer]), 'tp')]
    dot_general x16 -> x4, matrix products: 59 us -> 19.7 us  [the longest x2 15.3 us: local_fn(): jnp.einsum('sbkgd,bjkd->bksgj', q_rot, new_keys[layer], preferred_element...]
    pmax x5 -> x2, blocking collectives: 62.6 us -> 30.9 us  [local_fn(): glob_max = lax.pmax(loc_max, 'sp')]
  transfers between devices with their start and end apart: 15 -> 6, of which waited for: 13 -> 6; matrix products, arithmetic and copies ran while one was open for 8% -> 4% of each run, Pallas kernels for 0% -> 0%
where the time goes in v1:
time: 815 us; the launch traced here: 803 us
  waiting for transfers between devices  286 us (35%)
  local copies, waits for them, and re-layouts  250 us (31%)
  matrix products  191 us (23%)
  blocking collectives  30.9 us (4%)
  other arithmetic  29.3 us (4%)
  between operations  15.2 us (2%)
    dot_general x12, matrix products, project(): return jnp.dot(normed, weight, preferred_element_type=jnp.float32)  171 us
    psum x2, waiting for transfers between devices, local_fn(): proj_sum = lax.psum(project(attn_out, w_out[layer]), 'tp')  114 us
    dot_general x9, local copies, waits for them, and re-layouts, project(): return jnp.dot(normed, weight, preferred_element_type=jnp.float32)  102 us
    psum x2, waiting for transfers between devices, local_fn(): lax.psum(jnp.concatenate([loc_out, loc_sum], axis=-1) * jnp.exp(loc_max -...  91.3 us
    psum x2, waiting for transfers between devices, local_fn(): down_sum = lax.psum(project(mlp_act, w_down[layer]), 'tp')  80.8 us
    scatter x8, local copies, waits for them, and re-layouts, local_fn(): new_vals.at[layer, row_ids, write_slot[s]].set(v_vec[s], mode='drop')  37.8 us
    scatter x8, local copies, waits for them, and re-layouts, local_fn(): new_keys.at[layer, row_ids, write_slot[s]].set(k_rot[s], mode='drop')  37.8 us
    pmax x2, blocking collectives, local_fn(): glob_max = lax.pmax(loc_max, 'sp')  30.9 us
  transfers between devices with their start and end apart: 6, of which 6 were waited for; matrix products, arithmetic and copies ran while one was open for 4% of the time, Pallas kernels for 0%

profile of v1, /device:TPU:0, one launch (start us, length us, event | category | flops | bytes accessed | tf_op | source)
XLA Modules:
  0.0 803.2 jit_solution(13162051643048634374)
XLA Ops:
  7.2 12.1 %copy.170 = bf16[2,32,256,4,128]{4,3,2,1,0:T(4,128)(2,1)} copy(bf16[2,32,256,4,128]{4,3,2,1,0:T(4,128)(2,1)} %param.15) | data formatting | bytes 33554432
  23.9 6.2 copy.171
  31.2 5.7 slice_bitcast_fusion.3
  36.9 6.4 copy.79
  48.6 4.7 scatter_fusion
  53.2 4.8 scatter_fusion.1
  58.0 4.8 scatter_fusion.2
  62.8 4.7 scatter_fusion.3
  67.4 8.1 %slice.294 = bf16[1,32,256,4,128]{4,3,2,1,0:T(4,128)(2,1)} slice(bf16[2,32,256,4,128]{4,3,2,1,0:T(4,128)(2,1)} %scatter_fusion.3), slice={[0:1], [0:32], [0:256], [0:4], [0:128]} | slice | bytes 16777216 | tf_op jit(solution)/shard_map/slice | solution.py:63
  75.5 23.5 %slice_bitcast_fusion = (bf16[2048,4096]{0,1:T(8,128)(2,1)}, bf16[2048,4096]{0,1:T(8,128)(2,1)}) fusion(bf16[2,4096,2048]{2,1,0:T(8,128)(2,1)} %param.19), kind=kLoop, calls=%fused_computation.39 | loop fusion | bytes 67108864 | tf_op jit(solution)/shard_map/dot_general | solution.py:31
  99.0 20.9 %copy.74 = bf16[2048,4096]{1,0:T(8,128)(2,1)} copy(bf16[2048,4096]{0,1:T(8,128)(2,1)} %get-tuple-element.13) | data formatting | bytes 33554432 | tf_op jit(solution)/shard_map/dot_general | solution.py:31
  119.9 8.3 %fusion.119 = f32[128,16,128]{0,2,1:T(8,128)S(1)} fusion(bf16[128,4096,1]{1,0,2:T(8,128)(2,1)S(1)} %bitcast.232, bf16[16,128,4096]{2,1,0:T(8,128)(2,1)} %bitcast.228), kind=kOutput, calls=%fused_computation.218 | convolution fusion | flops 2147483648 | bytes 18874368 | tf_op jit(solution)/shard_map/dot_general | solution.py:31
  130.0 7.7 fusion.53
  137.6 16.5 %pmax.14 = f32[32,4,4,4,1]{3,2,1,0,4:T(4,128)S(1)} all-reduce(f32[32,4,4,4,1]{3,2,1,0,4:T(4,128)S(1)} %bitcast.236), channel_id=1, replica_groups=mesh['dp'=1,'tp'=2,'sp'=4] {'sp'}, use_global_device_ids=true, to_apply=%region_11.12 | all-reduce | flops 2048 | bytes 16384 | tf_op jit(solution)/shard_map/pmax | solution.py:69
  155.0 5.8 slice_bitcast_fusion.2
  160.8 6.4 copy.85
  171.0 4.7 scatter_fusion.4
  175.7 4.8 scatter_fusion.5
  180.5 4.8 scatter_fusion.6
  185.2 4.7 scatter_fusion.7
  189.9 5.5 slice.299
  207.2 46.0 %all-reduce.7.cloned.1.call-done = f32[32,4,4,4,129]{4,3,2,1,0:T(4,128)} async-done(((f32[32,4,4,4,129]{4,3,2,1,0:T(4,128)}), f32[32,4,4,4,129]{4,3,2,1,0:T(4,128)}) %all-reduce.7.cloned.1.call-update) | async-done | bytes 1056784 | tf_op jit(solution)/shard_map/psum | solution.py:70
  260.5 9.4 %fusion.20 = f32[128,4096]{1,0:T(8,128)} fusion(bf16[128,2048]{1,0:T(8,128)(2,1)S(1)} %reshape.337, bf16[2,2048,4096]{2,1,0:T(8,128)(2,1)} %param.22), kind=kOutput, calls=%fused_computation.36 | convolution fusion | flops 2147483648 | bytes 19398656 | tf_op jit(solution)/shard_map/dot_general | solution.py:31
  270.6 56.7 %all-reduce.9.cloned.1.call-done = f32[128,4096]{1,0:T(8,128)} async-done(((f32[128,4096]{1,0:T(8,128)}), f32[128,4096]{1,0:T(8,128)}) %all-reduce.9.cloned.1.call-update) | async-done | bytes 2097168 | tf_op jit(solution)/shard_map/psum | solution.py:73
  329.3 21.9 %fusion.10 = f32[128,7168]{1,0:T(8,128)} fusion(bf16[2,4096,7168]{2,1,0:T(8,128)(2,1)} %param.23, bf16[128,4096]{1,0:T(8,128)(2,1)S(1)} %get-tuple-element.11, f32[4096]{0:T(1024)S(1)} %bitcast.251, f32[128]{0:T(128)S(1)} %add_rsqrt_fusion.3), kind=kOutput, calls=%fused_computation.26 | convolution fusion | flops 7518289920 | bytes 63455744 | tf_op jit(solution)/shard_map/dot_general | solution.py:31
  351.2 40.0 %fusion.6 = f32[128,4096]{1,0:T(8,128)} fusion(bf16[2,7168,4096]{2,1,0:T(8,128)(2,1)} %param.25, bf16[2,4096,7168]{2,1,0:T(8,128)(2,1)} %param.24, f32[128,7168]{1,0:T(8,128)} %fusion.10, bf16[128,4096]{1,0:T(8,128)(2,1)S(1)} %get-tuple-element.11, f32[4096]{0:T(1024)S(1)} %bitcast.252, f32[128]{0:T(128)S(1)} %add_rsqrt_fusion.3), kind=kOutput, calls=%fused_computation.22 | convolution fusion | flops 15039987712 | bytes 124273152 | tf_op jit(solution)/shard_map/dot_general | solution.py:31
  391.3 6.6 copy.101
  397.9 20.7 %copy.96 = bf16[2048,4096]{1,0:T(8,128)(2,1)} copy(bf16[2048,4096]{0,1:T(8,128)(2,1)} %get-tuple-element.12) | data formatting | bytes 33554432 | tf_op jit(solution)/shard_map/dot_general | solution.py:31
  418.6 6.4 copy.107
  425.0 23.5 %all-reduce.11.cloned.1.call-done = f32[128,4096]{1,0:T(8,128)} async-done(((f32[128,4096]{1,0:T(8,128)}), f32[128,4096]{1,0:T(8,128)}) %all-reduce.11.cloned.1.call-update) | async-done | bytes 2097168 | tf_op jit(solution)/shard_map/psum | solution.py:77
  453.3 4.7 scatter_fusion.8
  458.0 4.8 scatter_fusion.9
  462.7 4.8 scatter_fusion.10
  467.5 4.7 scatter_fusion.11
  472.2 8.1 %slice.312 = bf16[1,32,256,4,128]{4,3,2,1,0:T(4,128)(2,1)} slice(bf16[2,32,256,4,128]{4,3,2,1,0:T(4,128)(2,1)} %scatter_fusion.11), slice={[1:2], [0:32], [0:256], [0:4], [0:128]} | slice | bytes 16777216 | tf_op jit(solution)/shard_map/slice | solution.py:63
  480.2 8.1 %fusion.64 = f32[128,16,128]{0,2,1:T(8,128)S(1)} fusion(bf16[16,128,4096]{2,1,0:T(8,128)(2,1)} %bitcast.227, bf16[128,4096]{1,0:T(8,128)(2,1)S(1)} %fusion.46), kind=kOutput, calls=%fused_computation.102 | convolution fusion | flops 2147483648 | bytes 18874368 | tf_op jit(solution)/shard_map/dot_general | solution.py:31
  489.9 7.6 fusion.54
  497.6 14.4 %pmax.15 = f32[32,4,4,4,1]{3,2,1,0,4:T(4,128)S(1)} all-reduce(f32[32,4,4,4,1]{3,2,1,0,4:T(4,128)S(1)} %bitcast.237), channel_id=1, replica_groups=mesh['dp'=1,'tp'=2,'sp'=4] {'sp'}, use_global_device_ids=true, to_apply=%region_27.28 | all-reduce | flops 2048 | bytes 16384 | tf_op jit(solution)/shard_map/pmax | solution.py:69
  516.6 4.7 scatter_fusion.12
  521.3 4.8 scatter_fusion.13
  526.1 4.8 scatter_fusion.14
  535.5 5.5 slice.317
  552.8 45.3 %all-reduce.13.cloned.1.call-done = f32[32,4,4,4,129]{4,3,2,1,0:T(4,128)} async-done(((f32[32,4,4,4,129]{4,3,2,1,0:T(4,128)}), f32[32,4,4,4,129]{4,3,2,1,0:T(4,128)}) %all-reduce.13.cloned.1.call-update) | async-done | bytes 1056784 | tf_op jit(solution)/shard_map/psum | solution.py:70
  605.1 9.4 %fusion.18 = f32[128,4096]{1,0:T(8,128)} fusion(bf16[128,2048]{1,0:T(8,128)(2,1)S(1)} %reshape.338, bf16[2,2048,4096]{2,1,0:T(8,128)(2,1)} %param.22), kind=kOutput, calls=%fused_computation.34 | convolution fusion | flops 2147483648 | bytes 19398656 | tf_op jit(solution)/shard_map/dot_general | solution.py:31
  614.6 57.3 %all-reduce.15.cloned.1.call-done = f32[128,4096]{1,0:T(8,128)} async-done(((f32[128,4096]{1,0:T(8,128)}), f32[128,4096]{1,0:T(8,128)}) %all-reduce.15.cloned.1.call-update) | async-done | bytes 2097168 | tf_op jit(solution)/shard_map/psum | solution.py:73
  673.9 21.9 %fusion.4 = f32[128,7168]{1,0:T(8,128)} fusion(bf16[2,4096,7168]{2,1,0:T(8,128)(2,1)} %param.23, bf16[128,4096]{1,0:T(8,128)(2,1)S(1)} %get-tuple-element.7, f32[4096]{0:T(1024)S(1)} %bitcast.249, f32[128]{0:T(128)S(1)} %add_rsqrt_fusion.1), kind=kOutput, calls=%fused_computation.20 | convolution fusion | flops 7518289920 | bytes 63455744 | tf_op jit(solution)/shard_map/dot_general | solution.py:31
  695.8 40.0 %fusion = f32[128,4096]{1,0:T(8,128)} fusion(bf16[2,7168,4096]{2,1,0:T(8,128)(2,1)} %param.25, bf16[2,4096,7168]{2,1,0:T(8,128)(2,1)} %param.24, f32[128,7168]{1,0:T(8,128)} %fusion.4, bf16[128,4096]{1,0:T(8,128)(2,1)S(1)} %get-tuple-element.7, f32[4096]{0:T(1024)S(1)} %bitcast.250, f32[128]{0:T(128)S(1)} %add_rsqrt_fusion.1), kind=kOutput, calls=%fused_computation.16 | convolution fusion | flops 15039987712 | bytes 124273152 | tf_op jit(solution)/shard_map/dot_general | solution.py:31
  735.9 57.3 %all-reduce.17.cloned.1.call-done = f32[128,4096]{1,0:T(8,128)} async-done(((f32[128,4096]{1,0:T(8,128)}), f32[128,4096]{1,0:T(8,128)}) %all-reduce.17.cloned.1.call-update) | async-done | bytes 2097168 | tf_op jit(solution)/shard_map/psum | solution.py:77
  (126 shorter events, 77.9 us)
Async XLA Ops:
  7.2 246.0 %all-reduce.7.cloned.1.call-start = ((), (), s32[]{:S(2)}) async-start(), calls=%async_computation | async-start | bytes 4194304 | tf_op jit(solution)/shard_map/psum | solution.py:70
  7.2 16.7 %copy-start = (bf16[2,32,256,4,128]{4,3,2,1,0:T(4,128)(2,1)S(1)}, bf16[2,32,256,4,128]{4,3,2,1,0:T(4,128)(2,1)}, u32[]{:S(2)}) copy-start(bf16[2,32,256,4,128]{4,3,2,1,0:T(4,128)(2,1)} %param.16) | copy-start | bytes 50331652
  23.9 6.2 copy-start.17
  23.9 6.4 copy-start.14
  23.9 7.0 copy-start.2
  43.5 84.8 %copy-start.9 = (f32[128,64]{0,1:T(8,128)}, f32[128,64]{0,1:T(8,128)S(1)}, u32[]{:S(2)}) copy-start(f32[128,64]{0,1:T(8,128)S(1)} %get-tuple-element.54) | copy-start | bytes 98308
  43.5 84.8 %copy-start.11 = (f32[128,64]{0,1:T(8,128)}, f32[128,64]{0,1:T(8,128)S(1)}, u32[]{:S(2)}) copy-start(f32[128,64]{0,1:T(8,128)S(1)} %get-tuple-element.55) | copy-start | bytes 98308
  189.9 5.5 copy-start.7
  207.1 120.1 %all-reduce.9.cloned.1.call-start = ((), (), s32[]{:S(2)}) async-start(), calls=%async_computation.1 | async-start | bytes 4194304 | tf_op jit(solution)/shard_map/psum | solution.py:73
  260.5 9.5 %copy-start.15 = (bf16[2,4096]{1,0:T(2,128)(2,1)S(1)}, bf16[2,4096]{1,0:T(2,128)(2,1)}, u32[]{:S(2)}) copy-start(bf16[2,4096]{1,0:T(2,128)(2,1)} %param.18) | copy-start | bytes 49156
  269.9 178.6 %all-reduce.11.cloned.1.call-start = ((), (), s32[]{:S(2)}) async-start(), calls=%async_computation.2 | async-start | bytes 4194304 | tf_op jit(solution)/shard_map/psum | solution.py:77
  391.2 206.8 %all-reduce.13.cloned.1.call-start = ((), (), s32[]{:S(2)}) async-start(), calls=%async_computation.3 | async-start | bytes 4194304 | tf_op jit(solution)/shard_map/psum | solution.py:70
  425.0 25.7 %copy-start.13 = (f32[1,4096]{1,0:T(1,128)S(1)}, f32[1,4096]{1,0:T(1,128)}, u32[]{:S(2)}) copy-start(f32[1,4096]{1,0:T(1,128)} %get-tuple-element.44) | copy-start | bytes 49156
  448.5 2.8 copy-start.1
  450.6 1.9 copy-start.10
  450.6 1.9 copy-start.12
  450.7 2.6 copy-start.6
  451.0 6.9 copy-start.5
  451.0 11.7 %copy-start.4 = (s32[32]{0:T(128)S(1)}, s32[32]{0:T(128)}, u32[]{:S(2)}) copy-start(s32[32]{0:T(128)} %get-tuple-element.51) | copy-start | bytes 388
  451.0 16.5 %copy-start.3 = (s32[32]{0:T(128)S(1)}, s32[32]{0:T(128)}, u32[]{:S(2)}) copy-start(s32[32]{0:T(128)} %get-tuple-element.46) | copy-start | bytes 388
  535.5 5.5 copy-start.8
  552.8 119.2 %all-reduce.15.cloned.1.call-start = ((), (), s32[]{:S(2)}) async-start(), calls=%async_computation.4 | async-start | bytes 4194304 | tf_op jit(solution)/shard_map/psum | solution.py:73
  614.5 59.4 %copy-start.16 = (f32[1,4096]{1,0:T(1,128)S(1)}, f32[1,4096]{1,0:T(1,128)}, u32[]{:S(2)}) copy-start(f32[1,4096]{1,0:T(1,128)} %get-tuple-element.42) | copy-start | bytes 49156
  614.6 178.6 %all-reduce.17.cloned.1.call-start = ((), (), s32[]{:S(2)}) async-start(), calls=%async_computation.5 | async-start | bytes 4194304 | tf_op jit(solution)/shard_map/psum | solution.py:77
Sparse Core Ops, SparseCore 0:
  207.2 45.9 all-reduce.6
  270.0 57.1 all-reduce.8
  391.4 57.0 all-reduce.10
  552.9 45.1 all-reduce.12
  614.7 57.1 all-reduce.14
  736.0 57.0 all-reduce.16

commit v2 on v1

v2 whole, which is shorter than its diff:
```python
import functools

import jax
import jax.numpy as jnp
from jax import lax
from jax.experimental import pallas as pl
from jax.experimental.pallas import tpu as pltpu
from jax.sharding import PartitionSpec as P

EPS = 1e-5
ROPE_BASE = 500000.0
F32 = jnp.float32
BF16 = jnp.bfloat16
MESH = pl.DeviceIdType.MESH
PC = 256
LOG2E = 1.4426950408889634


def rope_tables(positions, head_dim):
    half_dim = head_dim // 2
    inv_freq = 1.0 / (ROPE_BASE ** (jnp.arange(half_dim).astype(F32) * 2.0 / head_dim))
    angles = positions.astype(F32)[:, None] * inv_freq[None, :]
    cos_a, sin_a = jnp.cos(angles), jnp.sin(angles)
    return jnp.concatenate([cos_a, cos_a], -1), jnp.concatenate([-sin_a, sin_a], -1)


def qkv_kernel(u_ref, gain_ref, cos_ref, sin_ref, wq_ref, wk_ref, wv_ref, q_ref, k_ref, v_ref, h_scr):
    hd = cos_ref.shape[1]
    d_model = u_ref.shape[1]

    @pl.when(pl.program_id(0) == 0)
    def _():
        x = u_ref[...].astype(F32)
        inv = lax.rsqrt(jnp.sum(x * x, axis=-1, keepdims=True) * (1.0 / d_model) + EPS)
        h_scr[...] = (x * inv * gain_ref[...].astype(F32)).astype(BF16)

    h = h_scr[...]
    cos_a, sin_a = cos_ref[...], sin_ref[...]

    def rot(x):
        return (x * cos_a + pltpu.roll(x, hd // 2, 1) * sin_a).astype(BF16)

    q = jnp.dot(h, wq_ref[0], preferred_element_type=F32)
    for j in range(q_ref.shape[0]):
        q_ref[j] = rot(q[:, j * hd:(j + 1) * hd]).astype(F32)
    k = jnp.dot(h, wk_ref[0], preferred_element_type=F32)
    k_ref[0] = rot(k)
    v = jnp.dot(h, wv_ref[0], preferred_element_type=F32)
    v_ref[0] = v.astype(BF16)


def qkv_call(layer, u, gain, cos_a, sin_a, wq, wk, wv, hd):
    rows, d_model = u.shape
    kv_loc = wk.shape[2] // hd
    heads = wq.shape[2] // hd
    grp = heads // kv_loc
    full = lambda shape: pl.BlockSpec(shape, lambda j: (0,) * len(shape))
    return pl.pallas_call(
        qkv_kernel,
        grid=(kv_loc,),
        in_specs=[
            full((rows, d_model)), full((1, d_model)), full((rows, hd)), full((rows, hd)),
            pl.BlockSpec((1, d_model, grp * hd), lambda j: (layer, 0, j)),
            pl.BlockSpec((1, d_model, hd), lambda j: (layer, 0, j)),
            pl.BlockSpec((1, d_model, hd), lambda j: (layer, 0, j)),
        ],
        out_specs=[
            pl.BlockSpec((grp, rows, hd), lambda j: (j, 0, 0)),
            pl.BlockSpec((1, rows, hd), lambda j: (j, 0, 0)),
            pl.BlockSpec((1, rows, hd), lambda j: (j, 0, 0)),
        ],
        out_shape=[
            jax.ShapeDtypeStruct((heads, rows, hd), F32),
            jax.ShapeDtypeStruct((kv_loc, rows, hd), BF16),
            jax.ShapeDtypeStruct((kv_loc, rows, hd), BF16),
        ],
        scratch_shapes=[pltpu.VMEM((rows, d_model), BF16)],
        compiler_params=pltpu.CompilerParams(vmem_limit_bytes=60 * 2**20),
        name=f'qkv{layer}',
    )(u, gain, cos_a, sin_a, wq, wk, wv)


def attn_kernel(n_kv, n_steps, sp_size, has_prev, meta, q_ref, kn_ref, vn_ref, k_ref, v_ref, *rest):
    if has_prev:
        rest = rest[2:]
    ko_ref, vo_ref, o_ref, sm_ref, sl_ref, code = rest
    pair = pl.program_id(0)
    n_batch = pl.num_programs(0) * 2
    my_sp = meta[n_batch]
    heads, r8, hd = q_ref.shape
    rows = heads * r8
    n_cols = k_ref.shape[2]
    row_kv = rows // n_kv

    @pl.when(pair == 0)
    def _():
        ri = lax.broadcasted_iota(jnp.int32, (rows, n_cols), 0)
        ci = lax.broadcasted_iota(jnp.int32, (rows, n_cols), 1)
        same = (ci % n_kv) == (ri // row_kv)
        code[...] = jnp.where(same, (ci // n_kv) * sp_size + my_sp, 2**30)
        sm_ref[...] = jnp.zeros_like(sm_ref)
        sl_ref[...] = jnp.zeros_like(sl_ref)

    for b in range(2):
        ko_ref[0, b] = k_ref[0, b]
        vo_ref[0, b] = v_ref[0, b]
        length = meta[2 * pair + b]
        step = lax.rem(my_sp - lax.rem(length, sp_size) + sp_size, sp_size)
        slot = lax.div(length + step, sp_size)
        per = 16 // n_kv
        base = pl.multiple_of(lax.div(slot, per) * 16, 16)
        sub = lax.rem(slot, per)
        mine = lax.broadcasted_iota(jnp.int32, (16, hd), 0) // n_kv == sub
        ko_ref[0, b, pl.ds(base, 16), :] = jnp.where(mine, kn_ref[b], k_ref[0, b, pl.ds(base, 16), :])
        vo_ref[0, b, pl.ds(base, 16), :] = jnp.where(mine, vn_ref[b], v_ref[0, b, pl.ds(base, 16), :])

    q = q_ref[...].reshape(rows, hd)
    rcol = lax.broadcasted_iota(jnp.int32, (rows, 1), 0) % r8
    first = rcol < n_steps
    limit = jnp.where(first, meta[2 * pair], meta[2 * pair + 1]) + rcol % n_steps
    zero = jnp.zeros_like(q)
    q2 = jnp.concatenate([jnp.where(first, q, zero), jnp.where(first, zero, q)], axis=1).astype(BF16)
    k2 = jnp.concatenate([ko_ref[0, 0], ko_ref[0, 1]], axis=1)
    s = lax.dot_general(q2, k2, (((1,), (1,)), ((), ())), preferred_element_type=F32)
    s = jnp.where(code[...] <= limit, s * hd ** -0.5, -1e30)
    m = jnp.max(s, axis=-1, keepdims=True)
    p = jnp.exp(s - m)
    l = jnp.sum(p, axis=-1, keepdims=True)
    v2 = jnp.concatenate([vo_ref[0, 0], vo_ref[0, 1]], axis=1)
    o = jnp.dot(p.astype(BF16), v2, preferred_element_type=F32)
    o = jnp.where(first, o[:, :hd], o[:, hd:])
    o_ref[...] = o.reshape(heads, r8, hd)
    lane = lax.broadcasted_iota(jnp.int32, sm_ref.shape, 1)
    sm_ref[...] = jnp.where(lane == pair, m, sm_ref[...])
    sl_ref[...] = jnp.where(lane == pair, l, sl_ref[...])


def attn_call(layer, meta, q, kn, vn, kc, vc, prev, n_kv, n_steps, sp_size):
    n_layers, n_batch, n_cols, hd = kc.shape
    heads, rows, _ = q.shape
    r8 = 2 * n_steps
    srows = heads * r8
    cache = pl.BlockSpec((1, 2, n_cols, hd), lambda i, *_: (layer, i, 0, 0))
    in_specs = [
        pl.BlockSpec((heads, r8, hd), lambda i, *_: (0, i, 0)),
        pl.BlockSpec((2, 16, hd), lambda i, *_: (i, 0, 0)),
        pl.BlockSpec((2, 16, hd), lambda i, *_: (i, 0, 0)),
        cache, cache,
    ]
    args = [q, kn, vn, kc, vc]
    aliases = {}
    if prev is not None:
        in_specs += [pl.BlockSpec(memory_space=pl.ANY)] * 2
        args += list(prev)
        aliases = {6: 0, 7: 1}
    stat = pl.BlockSpec((srows, 128), lambda i, *_: (0, 0))
    return pl.pallas_call(
        functools.partial(attn_kernel, n_kv, n_steps, sp_size, prev is not None),
        grid_spec=pltpu.PrefetchScalarGridSpec(
            num_scalar_prefetch=1,
            grid=(n_batch // 2,),
            in_specs=in_specs,
            out_specs=[cache, cache, pl.BlockSpec((heads, r8, hd), lambda i, *_: (0, i, 0)), stat, stat],
            scratch_shapes=[pltpu.VMEM((srows, n_cols), jnp.int32)],
        ),
        out_shape=[
            jax.ShapeDtypeStruct(kc.shape, kc.dtype), jax.ShapeDtypeStruct(vc.shape, vc.dtype),
            jax.ShapeDtypeStruct((heads, rows, hd), F32),
            jax.ShapeDtypeStruct((srows, 128), F32), jax.ShapeDtypeStruct((srows, 128), F32),
        ],
        input_output_aliases=aliases,
        compiler_params=pltpu.CompilerParams(vmem_limit_bytes=40 * 2**20),
        name=f'attn{layer}',
    )(meta, *args)


def block_kernel(layer, o_ref, sm_ref, sl_ref, u_ref, gain_ref, wo_hbm, wg_hbm, wu_hbm, wd_hbm, out_ref,
                 wo_v, wg_v, wu_v, wd_v, part, g1, g2, h2, act, att,
                 r_d, r_x1, r_y1, r_x2, r_y2, r_o, r_st, mo_s, mo_k, mst, r_o2, r_st2,
                 wo_sem, wg_sem, wu_sem, wd_sem, m_send, m_recv, rs_send, rs_recv, ag_send, ag_recv):
    sp = lax.axis_index('sp')
    y = lax.axis_index('tp')
    c = lax.rem(sp, 2)
    x = lax.div(sp, 2)
    rows = u_ref.shape[0]
    d_model = u_ref.shape[1]
    hd = o_ref.shape[2]
    heads = o_ref.shape[0]
    n_pieces = d_model // PC
    f_loc = wd_v.shape[1]
    k_loc = wo_v.shape[1]
    n_f = wg_v.shape[0]
    core_dev = {'sp': 2 * x + 1 - c}
    x_dev = {'sp': 2 * (1 - x) + c}
    y_dev = {'tp': 1 - y}

    def piece(half, kind, far, sub):
        return half * 8 + kind * 4 + far * 2 + sub

    order = []
    for half in (1 - c, c):
        for kind, far in ((0, 1 - x), (1, 1 - y), (0, x), (1, y)):
            for sub in ((1 - y, y) if kind == 0 else (1 - x, x)):
                order.append(piece(half, kind, far, sub))

    copies = {}

    def start(key, src, dst, sem):
        cp = pltpu.make_async_copy(src, dst, sem)
        cp.start()
        copies[key] = cp

    rem_row = pl.multiple_of((8 * c + 4 * x) * hd, hd)
    for i in range(n_pieces):
        start(('o', i), wo_hbm.at[layer, pl.ds(rem_row, k_loc), pl.ds(pl.multiple_of(order[i] * PC, PC), PC)], wo_v.at[i], wo_sem.at[i])

    barrier = pltpu.get_barrier_semaphore()
    for dev in (core_dev, x_dev, y_dev):
        pl.semaphore_signal(barrier, inc=1, device_id=dev, device_id_type=MESH)
    pl.semaphore_wait(barrier, 3)

    def remote(src, dst, send, recv, dev):
        cp = pltpu.make_async_remote_copy(src_ref=src, dst_ref=dst, send_sem=send, recv_sem=recv, device_id=dev, device_id_type=MESH)
        cp.start()
        return cp

    hh = heads // 2
    hq = heads // 4
    sr = sm_ref.shape[0]
    away = 1 - c
    d_cp = [
        remote(sm_ref.at[pl.ds(pl.multiple_of(away * (sr // 2), 8), sr // 2)], r_st.at[0], m_send.at[0], m_recv.at[0], core_dev),
        remote(sl_ref.at[pl.ds(pl.multiple_of(away * (sr // 2), 8), sr // 2)], r_st.at[1], m_send.at[1], m_recv.at[1], core_dev),
        remote(o_ref.at[pl.ds(away * hh, hh)], r_o, m_send.at[2], m_recv.at[2], core_dev),
    ]

    f_off = pl.multiple_of(sp * f_loc, PC)
    for i in range(n_f):
        start(('g', i), wg_hbm.at[layer, :, pl.ds(pl.multiple_of(f_off + i * PC, PC), PC)], wg_v.at[i], wg_sem.at[i])
        start(('u', i), wu_hbm.at[layer, :, pl.ds(pl.multiple_of(f_off + i * PC, PC), PC)], wu_v.at[i], wu_sem.at[i])
    for i in range(n_pieces):
        start(('d', i), wd_hbm.at[layer, pl.ds(f_off, f_loc), pl.ds(pl.multiple_of(order[i] * PC, PC), PC)], wd_v.at[i], wd_sem.at[i])

    for cp in d_cp:
        cp.wait_recv()

    def merge_into(dst, st_dst, src_o, m1, l1, src_o2, m2, l2, n_heads):
        mx = jnp.maximum(m1, m2)
        f1 = jnp.exp(m1 - mx)
        f2 = jnp.exp(m2 - mx)
        ln = l1 * f1 + l2 * f2
        st_dst(mx, ln)
        for h in range(n_heads):
            for t in range(rows // 8):
                a = jnp.broadcast_to(f1[8 * h:8 * h + 8, t:t + 1], (8, hd))
                b = jnp.broadcast_to(f2[8 * h:8 * h + 8, t:t + 1], (8, hd))
                dst(h, t, src_o(h, t) * a + src_o2(h, t) * b, ln)

    def core_merge(q4, dst_o, slot):
        lo = pl.multiple_of(c * (sr // 2) + q4 * (sr // 4), 8)
        lr = pl.multiple_of(q4 * (sr // 4), 8)
        n = sr // 4

        def st_dst(mx, ln):
            mst[slot, 0] = mx
            mst[slot, 1] = ln

        def dst(h, t, val, ln):
            dst_o[h, 8 * t:8 * t + 8, :] = val

        merge_into(dst, st_dst,
                   lambda h, t: o_ref[c * hh + q4 * hq + h, 8 * t:8 * t + 8, :], sm_ref[pl.ds(lo, n)], sl_ref[pl.ds(lo, n)],
                   lambda h, t: r_o[q4 * hq + h, 8 * t:8 * t + 8, :], r_st[0, pl.ds(lr, n)], r_st[1, pl.ds(lr, n)], hq)

    core_merge(1 - x, mo_s, 0)
    x_cp = [
        remote(mst.at[0], r_st2, m_send.at[3], m_recv.at[3], x_dev),
        remote(mo_s, r_o2, m_send.at[4], m_recv.at[4], x_dev),
    ]
    core_merge(x, mo_k, 1)
    for cp in x_cp:
        cp.wait_recv()

    def fin(h, t, val, ln):
        den = jnp.broadcast_to(ln[8 * h:8 * h + 8, t:t + 1], (8, hd))
        mo_k[h, 8 * t:8 * t + 8, :] = val / den

    merge_into(fin, lambda mx, ln: None,
               lambda h, t: mo_k[h, 8 * t:8 * t + 8, :], mst[1, 0], mst[1, 1],
               lambda h, t: r_o2[h, 8 * t:8 * t + 8, :], r_st2[0], r_st2[1], hq)
    for h in range(hq):
        att[:, h * hd:(h + 1) * hd] = mo_k[h].astype(BF16)
    for cp in d_cp + x_cp:
        cp.wait_send()

    def all_reduce(product, resid, g):
        sends = []

        def rs(n, src, dst, dev):
            cp = remote(src, dst, rs_send.at[n], rs_recv.at[n], dev)
            sends.append(cp)
            return cp

        for k in range(4):
            for i in (2 * k, 2 * k + 1):
                part[i] = product(i)
            cp = rs(k, part.at[pl.ds(2 * k, 2)], r_d.at[pl.ds(2 * k, 2)], core_dev)
        waits = sends[:4]
        for k in range(4):
            for i in (2 * k, 2 * k + 1):
                part[8 + i] = product(8 + i)
            waits[k].wait_recv()
            for i in (2 * k, 2 * k + 1):
                part[8 + i] = part[8 + i] + r_d[i]
            if k == 0:
                a1 = rs(4, part.at[pl.ds(8, 2)], r_x1, x_dev)
            if k == 1:
                b1 = rs(5, part.at[pl.ds(10, 2)], r_y1, y_dev)
        a1.wait_recv()
        part[12] = part[12] + r_x1[0]
        a2 = rs(6, part.at[12], r_y2, y_dev)
        b1.wait_recv()
        part[14] = part[14] + r_y1[0]
        b2 = rs(7, part.at[14], r_x2, x_dev)
        part[13] = part[13] + r_x1[1]
        part[15] = part[15] + r_y1[1]

        gs = []

        def ag(n, p, dev):
            cp = remote(g.at[p], g.at[p], ag_send.at[n], ag_recv.at[n], dev)
            gs.append(cp)
            return cp

        pa = piece(c, 0, x, y)
        pb = piece(c, 1, y, x)
        a2.wait_recv()
        g[pa] = (resid(pa) + (part[13] + r_y2[...])).astype(BF16).astype(F32)
        ya = ag(0, pa, y_dev)
        xa = ag(1, pa, x_dev)
        d0 = ag(2, pa, core_dev)
        b2.wait_recv()
        g[pb] = (resid(pb) + (part[15] + r_x2[...])).astype(BF16).astype(F32)
        xb = ag(3, pb, x_dev)
        yb = ag(4, pb, y_dev)
        d1 = ag(5, pb, core_dev)
        ya.wait_recv()
        p = piece(c, 0, x, 1 - y)
        xf = ag(6, p, x_dev)
        d2 = ag(7, p, core_dev)
        xb.wait_recv()
        p = piece(c, 1, y, 1 - x)
        yf = ag(8, p, y_dev)
        d3 = ag(9, p, core_dev)
        xa.wait_recv()
        d4 = ag(10, piece(c, 0, 1 - x, y), core_dev)
        yb.wait_recv()
        d5 = ag(11, piece(c, 1, 1 - y, x), core_dev)
        xf.wait_recv()
        d6 = ag(12, piece(c, 0, 1 - x, 1 - y), core_dev)
        yf.wait_recv()
        d7 = ag(13, piece(c, 1, 1 - y, 1 - x), core_dev)
        for cp in (d0, d1, d2, d3, d4, d5, d6, d7):
            cp.wait_recv()
        for cp in sends + gs:
            cp.wait_send()

    def out_product(i):
        copies[('o', i)].wait()
        return jnp.dot(att[...], wo_v[i], preferred_element_type=F32)

    def u_resid(p):
        return u_ref[:, pl.ds(pl.multiple_of(p * PC, PC), PC)].astype(F32)

    all_reduce(out_product, u_resid, g1)

    sq = jnp.zeros((rows, PC), F32)
    for i in range(n_pieces):
        sq = sq + g1[i] * g1[i]
    inv = lax.rsqrt(jnp.sum(sq, axis=-1, keepdims=True) * (1.0 / d_model) + EPS)
    for i in range(n_pieces):
        h2[:, i * PC:(i + 1) * PC] = (g1[i] * inv * gain_ref[:, i * PC:(i + 1) * PC].astype(F32)).astype(BF16)

    for i in range(n_f):
        copies[('g', i)].wait()
        ga = jnp.dot(h2[...], wg_v[i], preferred_element_type=F32)
        copies[('u', i)].wait()
        up = jnp.dot(h2[...], wu_v[i], preferred_element_type=F32)
        act[:, i * PC:(i + 1) * PC] = (ga * jax.nn.sigmoid(ga) * up).astype(BF16)

    def down_product(i):
        copies[('d', i)].wait()
        return jnp.dot(act[...], wd_v[i], preferred_element_type=F32)

    all_reduce(down_product, lambda p: g1[p], g2)
    for i in range(n_pieces):
        out_ref[:, i * PC:(i + 1) * PC] = g2[i].astype(BF16)


def block_call(layer, o, sm, sl, u, gain, wo, wg, wu, wd, sp_size):
    rows, d_model = u.shape
    heads, _, hd = o.shape
    n_p = d_model // PC
    k_loc = wo.shape[1] // sp_size
    f_loc = wd.shape[1] // sp_size
    n_f = f_loc // PC
    sr = sm.shape[0]
    V = pltpu.VMEM
    dma = pltpu.SemaphoreType.DMA
    vm = pl.BlockSpec(memory_space=pltpu.VMEM)
    hbm = pl.BlockSpec(memory_space=pl.ANY)
    return pl.pallas_call(
        functools.partial(block_kernel, layer),
        out_shape=jax.ShapeDtypeStruct((rows, d_model), BF16),
        in_specs=[vm] * 5 + [hbm] * 4,
        out_specs=vm,
        scratch_shapes=[
            V((n_p, k_loc, PC), BF16), V((n_f, d_model, PC), BF16), V((n_f, d_model, PC), BF16), V((n_p, f_loc, PC), BF16),
            V((n_p, rows, PC), F32), V((n_p, rows, PC), F32), V((n_p, rows, PC), F32),
            V((rows, d_model), BF16), V((rows, f_loc), BF16), V((rows, k_loc), BF16),
            V((n_p // 2, rows, PC), F32), V((2, rows, PC), F32), V((2, rows, PC), F32), V((rows, PC), F32), V((rows, PC), F32),
            V((heads // 2, rows, hd), F32), V((2, sr // 2, 128), F32),
            V((heads // 4, rows, hd), F32), V((heads // 4, rows, hd), F32), V((2, 2, sr // 4, 128), F32),
            V((heads // 4, rows, hd), F32), V((2, sr // 4, 128), F32),
            dma((n_p,)), dma((n_f,)), dma((n_f,)), dma((n_p,)),
            dma((5,)), dma((5,)), dma((8,)), dma((8,)), dma((14,)), dma((14,)),
        ],
        compiler_params=pltpu.CompilerParams(collective_id=layer, has_side_effects=True, vmem_limit_bytes=67043328),
        name=f'block{layer}',
    )(o, sm, sl, u, gain, wo, wg, wu, wd)


def solution(mesh):
    sp_size = mesh.shape['sp']

    def local_fn(tok_emb, lengths, key_cache, val_cache, gain_attn, gain_mlp, w_query, w_key, w_value, w_out, w_gate, w_up, w_down):
        n_steps, n_batch, d_model = tok_emb.shape
        n_layers, _, loc_len, kv_loc, hd = key_cache.shape
        rows = n_steps * n_batch
        my_sp = lax.axis_index('sp').astype(jnp.int32)
        cur_pos = (lengths[:, None] + jnp.arange(n_steps)[None, :]).reshape(rows)
        cos_a, sin_a = rope_tables(cur_pos, hd)
        mine = (cur_pos % sp_size == my_sp).reshape(n_batch, n_steps)
        meta = jnp.concatenate([lengths, my_sp[None]])
        u = tok_emb.transpose(1, 0, 2).reshape(rows, d_model)
        kc = key_cache.reshape(n_layers, n_batch, loc_len * kv_loc, hd)
        vc = val_cache.reshape(n_layers, n_batch, loc_len * kv_loc, hd)

        def own_row(t):
            t = t.reshape(kv_loc, n_batch, n_steps, hd)
            t = jnp.sum(jnp.where(mine[None, :, :, None], t, jnp.zeros_like(t)), axis=2)
            return jnp.tile(t.transpose(1, 0, 2), (1, 16 // kv_loc, 1))

        prev = None
        for layer in range(n_layers):
            q, k, v = qkv_call(layer, u, gain_attn[layer][None], cos_a, sin_a, w_query, w_key, w_value, hd)
            nk, nv, o, sm, sl = attn_call(layer, meta, q, own_row(k), own_row(v), kc, vc, prev, kv_loc, n_steps, sp_size)
            prev = (nk, nv)
            u = block_call(layer, o, sm, sl, u, gain_mlp[layer][None], w_out, w_gate, w_up, w_down, sp_size)
        hidden = u.reshape(n_batch, n_steps, d_model).transpose(1, 0, 2)
        return hidden, prev[0].reshape(key_cache.shape), prev[1].reshape(val_cache.shape)

    cache_spec = P(None, 'dp', 'sp', 'tp', None)
    col_spec = P(None, None, 'tp')
    row_spec = P(None, 'tp', None)
    emb_spec = P(None, 'dp', None)
    return jax.shard_map(local_fn, mesh=mesh, in_specs=(emb_spec, P('dp'), cache_spec, cache_spec, P(), P(), col_spec, col_spec, col_spec, row_spec, col_spec, col_spec, row_spec), out_specs=(emb_spec, cache_spec, cache_spec), check_vma=False)
```

time: 815 us -> 251 us (0.31); the launches traced: 803 us -> 249 us
  waiting for transfers between devices: 286 us -> 0 us
  local copies, waits for them, and re-layouts: 250 us -> 16.3 us
  Pallas kernels: 0 us -> 226 us
  matrix products: 191 us -> 0 us
  blocking collectives: 30.9 us -> 0 us
  other arithmetic: 29.3 us -> 6.08 us
  between operations: 15.2 us -> 0.82 us
    psum x6 -> x0, waiting for transfers between devices: 286 us -> none  [the longest x2 114 us: local_fn(): proj_sum = lax.psum(project(attn_out, w_out[layer]), 'tp')]
    pallas_call x0 -> x6, Pallas kernels: none -> 226 us  [the longest x2 165 us: block_call(): pl.pallas_call(functools.partial(block_kernel, layer), out_shape=jax.Shap...]
    dot_general x16 -> x0, matrix products: 191 us -> none  [the longest x12 171 us: project(): return jnp.dot(normed, weight, preferred_element_type=jnp.float32)]
    dot_general x9 -> x0, local copies, waits for them, and re-layouts: 102 us -> none  [project(): return jnp.dot(normed, weight, preferred_element_type=jnp.float32)]
    scatter x16 -> x0, local copies, waits for them, and re-layouts: 75.6 us -> none  [the longest x8 37.8 us: local_fn(): new_vals.at[layer, row_ids, write_slot[s]].set(v_vec[s], mode='drop')]
    pmax x2 -> x0, blocking collectives: 30.9 us -> none  [local_fn(): glob_max = lax.pmax(loc_max, 'sp')]
    slice x14 -> x2, local copies, waits for them, and re-layouts: 30.5 us -> 2.87 us  [the longest x1 1.44 us: local_fn(): gain_attn[layer][None]]
    unnamed x38 -> x24, local copies, waits for them, and re-layouts: 23.1 us -> 6.94 us
  transfers between devices with their start and end apart: 6 -> 0, of which waited for: 6 -> 0; matrix products, arithmetic and copies ran while one was open for 4% -> 0% of each run, Pallas kernels for 0% -> 0%
where the time goes in v2:
time: 251 us; the launch traced here: 249 us
  Pallas kernels  226 us (90%)
  local copies, waits for them, and re-layouts  16.3 us (6%)
  other arithmetic  6.08 us (2%)
    pallas_call x2, Pallas kernels, block_call(): pl.pallas_call(functools.partial(block_kernel, layer), out_shape=jax.Shap...  165 us
    pallas_call x2, Pallas kernels, attn_call(): pl.pallas_call(functools.partial(attn_kernel, n_kv, n_steps, sp_size, pre...  36.7 us
    pallas_call x2, Pallas kernels, qkv_call(): pl.pallas_call(qkv_kernel, grid=(kv_loc,), in_specs=[full((rows, d_model)...  24.8 us
    unnamed x24, local copies, waits for them, and re-layouts  6.94 us

profile of v2, /device:TPU:0, one launch (start us, length us, event | category | flops | bytes accessed | tf_op | source)
XLA Modules:
  0.0 249.3 jit_solution(9845041895682653660)
XLA Ops:
  0.6 0.7 pad_add_fusion.meta
  1.4 0.0 copy-start.8
  1.4 0.7 fusion.2
  2.1 0.0 copy-start.10
  2.1 0.7 fusion.3
  2.9 0.1 convert_element_type.26
  3.0 1.4 fusion.8
  4.4 1.4 fusion.7
  5.8 0.3 fusion
  6.1 0.8 pad_maximum_fusion
  6.9 2.0 copy.22
  8.9 1.1 reshape.105.u_ref
  10.0 12.4 %qkv0.1 = (f32[16,128,128]{2,1,0:T(8,128)}, bf16[4,128,128]{2,1,0:T(8,128)(2,1)}, bf16[4,128,128]{2,1,0:T(8,128)(2,1)}) custom-call(bf16[128,4096]{1,0:T(8,128)(2,1)} %reshape.105.u_ref, bf16[1,4096]{1,0:T(2,128)(2,1)} %get-tuple-element.42.gain_ref, f32[128,128]{1,0:T(8,128)} %get-tuple-element.46.cos_ref, f32[128,128]{1,0:T(8,128)} %get-tuple-element.47.sin_ref, ...), custom_call_target="tpu_custom_call" | custom-call | tf_op jit(solution)/shard_map/qkv0/pallas_call | solution.py:58
  22.4 0.0 copy-done.10
  22.4 1.4 select_reduce_fusion.2
  24.0 0.0 copy-done.8
  24.0 0.0 copy-start.3
  24.0 1.2 copy-done.3
  25.2 18.4 %attn0.1 = (bf16[2,32,1024,128]{3,2,1,0:T(8,128)(2,1)}, bf16[2,32,1024,128]{3,2,1,0:T(8,128)(2,1)}, f32[16,128,128]{2,1,0:T(8,128)S(1)}, f32[128,128]{1,0:T(8,128)S(1)}, f32[128,128]{1,0:T(8,128)S(1)}) custom-call(s32[33]{0:T(128)S(1)} %pad_add_fusion.meta, f32[16,128,128]{2,1,0:T(8,128)S(1)} %copy-done.3, bf16[32,16,128]{2,1,0:T(8,128)(2,1)S(1)} %bitcast.23, ...), custom_call_target="tpu_custom_call" | custom-call | tf_op jit(solution)/shard_map/attn0/pallas_call | solution.py:157
  43.6 0.0 copy-start.2
  43.6 1.0 copy-done.2
  44.6 0.0 copy-start.6
  44.6 0.6 copy-done.6
  45.2 0.0 copy-start.7
  45.2 0.6 copy-done.7
  45.8 84.0 %block0.1.u_ref = bf16[128,4096]{1,0:T(8,128)(2,1)} custom-call(f32[16,128,128]{2,1,0:T(8,128)} %copy-done.2, f32[128,128]{1,0:T(8,128)} %copy-done.6, f32[128,128]{1,0:T(8,128)} %copy-done.7, bf16[128,4096]{1,0:T(8,128)(2,1)} %reshape.105.u_ref, bf16[1,4096]{1,0:T(2,128)(2,1)} %get-tuple-element.40.gain_ref, bf16[2,2048,4096]{2,1,0:T(8,128)(2,1)} %wo_hbm.3, ...), custom_call_target="tpu_custom_call" | custom-call | tf_op jit(solution)/shard_map/block0/pallas_call | solution.py:412
  129.8 0.0 copy-start.11
  129.9 0.0 copy-start.9
  129.9 12.4 %qkv1.1 = (f32[16,128,128]{2,1,0:T(8,128)}, bf16[4,128,128]{2,1,0:T(8,128)(2,1)}, bf16[4,128,128]{2,1,0:T(8,128)(2,1)}) custom-call(bf16[128,4096]{1,0:T(8,128)(2,1)} %block0.1.u_ref, bf16[1,4096]{1,0:T(2,128)(2,1)} %get-tuple-element.41.gain_ref, f32[128,128]{1,0:T(8,128)} %get-tuple-element.46.cos_ref, f32[128,128]{1,0:T(8,128)} %get-tuple-element.47.sin_ref, ...), custom_call_target="tpu_custom_call" | custom-call | tf_op jit(solution)/shard_map/qkv1/pallas_call | solution.py:58
  142.3 0.0 copy-done.11
  142.3 1.4 select_reduce_fusion
  143.8 0.0 copy-done.9
  143.8 0.0 copy-start
  143.9 1.2 copy-done
  145.1 18.4 %attn1.1 = (bf16[2,32,1024,128]{3,2,1,0:T(8,128)(2,1)}, bf16[2,32,1024,128]{3,2,1,0:T(8,128)(2,1)}, f32[16,128,128]{2,1,0:T(8,128)S(1)}, f32[128,128]{1,0:T(8,128)S(1)}, f32[128,128]{1,0:T(8,128)S(1)}) custom-call(s32[33]{0:T(128)S(1)} %copy-done.9, f32[16,128,128]{2,1,0:T(8,128)S(1)} %copy-done, ...), custom_call_target="tpu_custom_call", output_to_operand_aliasing={{0}: (6, {}), {1}: (7, {})} | custom-call | tf_op jit(solution)/shard_map/attn1/pallas_call | solution.py:157
  163.4 0.0 copy-start.1
  163.4 1.0 copy-done.1
  164.4 0.0 copy-start.4
  164.4 0.6 copy-done.4
  165.0 0.0 copy-start.5
  165.0 0.6 copy-done.5
  165.7 80.6 %block1.1 = bf16[128,4096]{1,0:T(8,128)(2,1)} custom-call(f32[16,128,128]{2,1,0:T(8,128)} %copy-done.1, f32[128,128]{1,0:T(8,128)} %copy-done.4, f32[128,128]{1,0:T(8,128)} %copy-done.5, bf16[128,4096]{1,0:T(8,128)(2,1)} %block0.1.u_ref, bf16[1,4096]{1,0:T(2,128)(2,1)} %get-tuple-element.39.gain_ref, bf16[2,2048,4096]{2,1,0:T(8,128)(2,1)} %wo_hbm.3, ...), custom_call_target="tpu_custom_call" | custom-call | tf_op jit(solution)/shard_map/block1/pallas_call | solution.py:412
  246.3 1.5 reshape.112
  247.7 1.6 copy.29
  (9 shorter events, 0.2 us)
Async XLA Ops:
  1.4 22.6 %copy-start.8 = (s32[33]{0:T(128)}, s32[33]{0:T(128)S(1)}, u32[]{:S(2)}) copy-start(s32[33]{0:T(128)S(1)} %pad_add_fusion.meta) | copy-start | bytes 400
  2.1 20.3 %copy-start.10 = (pred[32,4]{1,0:T(8,128)(4,1)}, pred[32,4]{1,0:T(8,128)(4,1)S(1)}, u32[]{:S(2)}) copy-start(pred[32,4]{1,0:T(8,128)(4,1)S(1)} %fusion.2) | copy-start | bytes 388
  24.0 1.2 copy-start.3
  43.6 1.0 copy-start.2
  44.6 0.6 copy-start.6
  45.2 0.6 copy-start.7
  129.8 12.4 %copy-start.11 = (pred[32,4]{1,0:T(8,128)(4,1)S(1)}, pred[32,4]{1,0:T(8,128)(4,1)}, u32[]{:S(2)}) copy-start(pred[32,4]{1,0:T(8,128)(4,1)} %copy-done.10) | copy-start | bytes 388
  129.9 14.0 %copy-start.9 = (s32[33]{0:T(128)S(1)}, s32[33]{0:T(128)}, u32[]{:S(2)}) copy-start(s32[33]{0:T(128)} %copy-done.8) | copy-start | bytes 400
  143.8 1.2 copy-start
  163.4 1.0 copy-start.1
  164.4 0.6 copy-start.4
  165.0 0.6 copy-start.5

commit v3 on v2

v3 whole, which is shorter than its diff:
```python
import functools

import jax
import jax.numpy as jnp
import numpy as np
from jax import lax
from jax.experimental import pallas as pl
from jax.experimental.pallas import tpu as pltpu
from jax.sharding import PartitionSpec as P

EPS = 1e-5
ROPE_BASE = 500000.0
F32 = jnp.float32
BF16 = jnp.bfloat16
MESH = pl.DeviceIdType.MESH
PC = 256
VMEM_ALL = 67043328


def rope_table(first_pos, n_pos, head_dim):
    half = head_dim // 2
    inv_freq = (1.0 / (np.float32(ROPE_BASE) ** (np.arange(half).astype(np.float32) * np.float32(2.0 / head_dim)))).astype(np.float32)
    pos = np.arange(first_pos, first_pos + n_pos).astype(np.float32)
    angles = (pos[:, None] * inv_freq[None, :]).astype(np.float32)
    return np.concatenate([np.cos(angles), np.sin(angles)], axis=1).astype(np.float32)


def permutation(rows, n_steps, to_batch_major):
    ri = lax.broadcasted_iota(jnp.int32, (rows, rows), 0)
    ci = lax.broadcasted_iota(jnp.int32, (rows, rows), 1)
    n_batch = rows // n_steps
    if to_batch_major:
        src = (ri % n_steps) * n_batch + ri // n_steps
    else:
        src = (ri % n_batch) * n_steps + ri // n_batch
    return jnp.where(ci == src, 1.0, 0.0).astype(BF16)


def qkv_kernel(layer, n_steps, first_pos, first, *refs):
    if first:
        len_ref, tab_ref, u_ref, gain_ref, wq_ref, wk_ref, wv_ref, q_ref, k_ref, v_ref, cos_ref, sin_ref, up_ref, h_scr = refs
    else:
        u_ref, gain_ref, cos_ref, sin_ref, wq_ref, wk_ref, wv_ref, q_ref, k_ref, v_ref, h_scr = refs
    rows, d_model = u_ref.shape
    hd = cos_ref.shape[1]

    @pl.when(pl.program_id(0) == 0)
    def _():
        x = u_ref[...].astype(F32)
        inv = lax.rsqrt(jnp.sum(x * x, axis=-1, keepdims=True) * (1.0 / d_model) + EPS)
        h = (x * inv * gain_ref[layer:layer + 1, :].astype(F32)).astype(BF16)
        if first:
            perm = permutation(rows, n_steps, True)
            h_scr[...] = jnp.dot(perm, h, preferred_element_type=F32).astype(BF16)
            up_ref[...] = jnp.dot(perm, u_ref[...], preferred_element_type=F32).astype(BF16)
            for b in range(rows // n_steps):
                cos_ref[b * n_steps:(b + 1) * n_steps, :] = tab_ref[pl.ds(len_ref[b] - first_pos, n_steps), :]
            both = cos_ref[...]
            swap = pltpu.roll(both, hd // 2, 1)
            low = lax.broadcasted_iota(jnp.int32, both.shape, 1) < hd // 2
            cos_ref[...] = jnp.where(low, both, swap)
            sin_ref[...] = jnp.where(low, -swap, both)
        else:
            h_scr[...] = h

    h = h_scr[...]
    cos_a, sin_a = cos_ref[...], sin_ref[...]

    def rot(x):
        return (x * cos_a + pltpu.roll(x, hd // 2, 1) * sin_a).astype(BF16).astype(F32)

    q = jnp.dot(h, wq_ref[0], preferred_element_type=F32)
    for j in range(q_ref.shape[0]):
        q_ref[j] = rot(q[:, j * hd:(j + 1) * hd])
    k = jnp.dot(h, wk_ref[0], preferred_element_type=F32)
    k_ref[0] = rot(k)
    v = jnp.dot(h, wv_ref[0], preferred_element_type=F32)
    v_ref[0] = v.astype(BF16).astype(F32)


def qkv_call(layer, u, gain, rope, lengths, wq, wk, wv, n_steps, hd, first_pos):
    rows, d_model = u.shape
    kv_loc = wk.shape[2] // hd
    heads = wq.shape[2] // hd
    grp = heads // kv_loc
    first = layer == 0
    full = lambda shape: pl.BlockSpec(shape, lambda j: (0,) * len(shape))
    weights = [
        pl.BlockSpec((1, d_model, grp * hd), lambda j: (layer, 0, j)),
        pl.BlockSpec((1, d_model, hd), lambda j: (layer, 0, j)),
        pl.BlockSpec((1, d_model, hd), lambda j: (layer, 0, j)),
    ]
    out_specs = [
        pl.BlockSpec((grp, rows, hd), lambda j: (j, 0, 0)),
        pl.BlockSpec((1, rows, hd), lambda j: (j, 0, 0)),
        pl.BlockSpec((1, rows, hd), lambda j: (j, 0, 0)),
    ]
    out_shape = [
        jax.ShapeDtypeStruct((heads, rows, hd), F32),
        jax.ShapeDtypeStruct((kv_loc, rows, hd), F32),
        jax.ShapeDtypeStruct((kv_loc, rows, hd), F32),
    ]
    if first:
        args = [lengths, rope, u, gain, wq, wk, wv]
        in_specs = [pl.BlockSpec(memory_space=pltpu.SMEM), full(rope.shape), full(u.shape), full(gain.shape)] + weights
        out_specs += [full((rows, hd)), full((rows, hd)), full((rows, d_model))]
        out_shape += [jax.ShapeDtypeStruct((rows, hd), F32)] * 2 + [jax.ShapeDtypeStruct((rows, d_model), BF16)]
    else:
        args = [u, gain, *rope, wq, wk, wv]
        in_specs = [full(u.shape), full(gain.shape), full((rows, hd)), full((rows, hd))] + weights
    return pl.pallas_call(
        functools.partial(qkv_kernel, layer, n_steps, first_pos, first),
        grid=(kv_loc,),
        in_specs=in_specs,
        out_specs=out_specs,
        out_shape=out_shape,
        scratch_shapes=[pltpu.VMEM((rows, d_model), BF16)],
        compiler_params=pltpu.CompilerParams(vmem_limit_bytes=VMEM_ALL),
        name=f'qkv{layer}',
    )(*args)


SEQS = 4
SLOTS = 6
AHEAD = 4


def attn_kernel(layer, n_kv, n_steps, sp_size, has_prev, len_ref, q_ref, kn_ref, vn_ref, k_hbm, v_hbm, *rest):
    if has_prev:
        rest = rest[2:]
    ko_hbm, vo_hbm, o_ref, sm_ref, sl_ref, code, kb, vb, in_sem, out_sem = rest
    my_sp = lax.axis_index('sp').astype(jnp.int32)
    heads, all_rows, hd = q_ref.shape
    n_batch = all_rows // n_steps
    n_iter = n_batch // SEQS
    r8 = 2 * n_steps
    rows = heads * r8
    n_cols = kb.shape[2]
    row_kv = rows // n_kv

    def reads(i):
        slot = lax.rem(i, SLOTS)
        src = pl.ds(i * SEQS, SEQS)
        return (pltpu.make_async_copy(k_hbm.at[layer, src], kb.at[slot], in_sem.at[slot, 0]),
                pltpu.make_async_copy(v_hbm.at[layer, src], vb.at[slot], in_sem.at[slot, 1]))

    def writes(i):
        slot = lax.rem(i, SLOTS)
        dst = pl.ds(i * SEQS, SEQS)
        return (pltpu.make_async_copy(kb.at[slot], ko_hbm.at[layer, dst], out_sem.at[slot, 0]),
                pltpu.make_async_copy(vb.at[slot], vo_hbm.at[layer, dst], out_sem.at[slot, 1]))

    for i in range(AHEAD):
        for cp in reads(i):
            cp.start()

    ri = lax.broadcasted_iota(jnp.int32, (rows, n_cols), 0)
    ci = lax.broadcasted_iota(jnp.int32, (rows, n_cols), 1)
    same = (ci % n_kv) == (ri // row_kv)
    code[...] = jnp.where(same, (ci // n_kv) * sp_size + my_sp, 2**30)
    sm_ref[...] = jnp.zeros_like(sm_ref)
    sl_ref[...] = jnp.zeros_like(sl_ref)
    rcol = lax.broadcasted_iota(jnp.int32, (rows, 1), 0) % r8
    first = rcol < n_steps
    row16 = lax.broadcasted_iota(jnp.int32, (16, hd), 0)
    lane = lax.broadcasted_iota(jnp.int32, sm_ref.shape, 1)
    per = 16 // n_kv

    def body(i, _):
        slot_b = lax.rem(i, SLOTS)
        for cp in reads(i):
            cp.wait()
        for b in range(SEQS):
            seq = i * SEQS + b
            length = len_ref[seq]
            step = lax.rem(my_sp - lax.rem(length, sp_size) + sp_size, sp_size)
            slot = lax.div(length + step, sp_size)
            base = pl.multiple_of(lax.div(slot, per) * 16, 16)
            mine = row16 // n_kv == lax.rem(slot, per)
            new_row = seq * n_steps + step
            for buf, src in ((kb, kn_ref), (vb, vn_ref)):
                fresh = jnp.broadcast_to(src[0, pl.ds(new_row, 1), :], (16, hd))
                for j in range(1, n_kv):
                    fresh = jnp.where(row16 % n_kv == j, jnp.broadcast_to(src[j, pl.ds(new_row, 1), :], (16, hd)), fresh)
                old = buf[slot_b, b, pl.ds(base, 16), :]
                buf[slot_b, b, pl.ds(base, 16), :] = jnp.where(mine, fresh, old.astype(F32)).astype(BF16)
        for cp in writes(i):
            cp.start()
        sm, sl = sm_ref[...], sl_ref[...]
        for t in range(SEQS // 2):
            pair = i * (SEQS // 2) + t
            r0 = pl.multiple_of(pair * r8, r8)
            q = q_ref[:, pl.ds(r0, r8), :].reshape(rows, hd)
            limit = jnp.where(first, len_ref[2 * pair], len_ref[2 * pair + 1]) + rcol % n_steps
            zero = jnp.zeros_like(q)
            q2 = jnp.concatenate([jnp.where(first, q, zero), jnp.where(first, zero, q)], axis=1).astype(BF16)
            k2 = jnp.concatenate([kb[slot_b, 2 * t], kb[slot_b, 2 * t + 1]], axis=1)
            s = lax.dot_general(q2, k2, (((1,), (1,)), ((), ())), preferred_element_type=F32)
            s = jnp.where(code[...] <= limit, s * hd ** -0.5, -1e30)
            m = jnp.max(s, axis=-1, keepdims=True)
            p = jnp.exp(s - m)
            l = jnp.sum(p, axis=-1, keepdims=True)
            v2 = jnp.concatenate([vb[slot_b, 2 * t], vb[slot_b, 2 * t + 1]], axis=1)
            o = jnp.dot(p.astype(BF16), v2, preferred_element_type=F32)
            o = jnp.where(first, o[:, :hd], o[:, hd:])
            o_ref[:, pl.ds(r0, r8), :] = o.reshape(heads, r8, hd)
            sm = jnp.where(lane == pair, m, sm)
            sl = jnp.where(lane == pair, l, sl)
        sm_ref[...] = sm
        sl_ref[...] = sl

        @pl.when(i + AHEAD >= SLOTS)
        def _():
            for cp in writes(i + AHEAD - SLOTS):
                cp.wait()

        @pl.when(i + AHEAD < n_iter)
        def _():
            for cp in reads(i + AHEAD):
                cp.start()
        return 0

    lax.fori_loop(0, n_iter, body, 0)
    for i in range(n_iter + AHEAD - SLOTS, n_iter):
        for cp in writes(i):
            cp.wait()


def attn_call(layer, lengths, q, kn, vn, kc, vc, prev, n_kv, n_steps, sp_size):
    n_layers, n_batch, n_cols, hd = kc.shape
    heads, rows, _ = q.shape
    srows = heads * 2 * n_steps
    vm = pl.BlockSpec(memory_space=pltpu.VMEM)
    hbm = pl.BlockSpec(memory_space=pl.ANY)
    in_specs = [pl.BlockSpec(memory_space=pltpu.SMEM), vm, vm, vm, hbm, hbm]
    args = [lengths, q, kn, vn, kc, vc]
    aliases = {}
    if prev is not None:
        in_specs += [hbm, hbm]
        args += list(prev)
        aliases = {6: 0, 7: 1}
    return pl.pallas_call(
        functools.partial(attn_kernel, layer, n_kv, n_steps, sp_size, prev is not None),
        in_specs=in_specs,
        out_specs=[hbm, hbm, vm, vm, vm],
        out_shape=[
            jax.ShapeDtypeStruct(kc.shape, kc.dtype), jax.ShapeDtypeStruct(vc.shape, vc.dtype),
            jax.ShapeDtypeStruct((heads, rows, hd), F32),
            jax.ShapeDtypeStruct((srows, 128), F32), jax.ShapeDtypeStruct((srows, 128), F32),
        ],
        scratch_shapes=[
            pltpu.VMEM((srows, n_cols), jnp.int32),
            pltpu.VMEM((SLOTS, SEQS, n_cols, hd), BF16), pltpu.VMEM((SLOTS, SEQS, n_cols, hd), BF16),
            pltpu.SemaphoreType.DMA((SLOTS, 2)), pltpu.SemaphoreType.DMA((SLOTS, 2)),
        ],
        input_output_aliases=aliases,
        compiler_params=pltpu.CompilerParams(vmem_limit_bytes=VMEM_ALL),
        name=f'attn{layer}',
    )(*args)


def block_kernel(layer, last, n_steps, o_ref, sm_ref, sl_ref, u_ref, gain_ref, wo_hbm, wg_hbm, wu_hbm, wd_hbm, *refs):
    has_next = not last
    if has_next:
        gain_a_ref, cos_ref, sin_ref, wq_hbm, wk_hbm, wv_hbm, out_ref, q_ref, k_ref, v_ref, *refs = refs
    else:
        out_ref, *refs = refs
    block_body(layer, last, n_steps, has_next, o_ref, sm_ref, sl_ref, u_ref, gain_ref, wo_hbm, wg_hbm, wu_hbm, wd_hbm,
               (gain_a_ref, cos_ref, sin_ref, wq_hbm, wk_hbm, wv_hbm) if has_next else None, out_ref,
               (q_ref, k_ref, v_ref) if has_next else None, *refs)


def block_body(layer, last, n_steps, has_next, o_ref, sm_ref, sl_ref, u_ref, gain_ref, wo_hbm, wg_hbm, wu_hbm, wd_hbm, nxt, out_ref, qkv,
                 wo_v, wg_v, wu_v, wd_v, part, g1, g2, h2, act, att,
                 r_d, r_x1, r_y1, r_x2, r_y2, r_o, r_st, mo_s, mo_k, mst, r_o2, r_st2,
                 wo_sem, wg_sem, wu_sem, wd_sem, m_send, m_recv, rs_send, rs_recv, ag_send, ag_recv):
    if has_next:
        gain_a_ref, cos_ref, sin_ref, wq_hbm, wk_hbm, wv_hbm = nxt
        q_ref, k_ref, v_ref = qkv
    sp = lax.axis_index('sp')
    y = lax.axis_index('tp')
    c = lax.rem(sp, 2)
    x = lax.div(sp, 2)
    rows = u_ref.shape[0]
    d_model = u_ref.shape[1]
    hd = o_ref.shape[2]
    heads = o_ref.shape[0]
    n_pieces = d_model // PC
    f_loc = wd_v.shape[1]
    k_loc = wo_v.shape[1]
    n_f = wg_v.shape[0]
    core_dev = {'sp': 2 * x + 1 - c}
    x_dev = {'sp': 2 * (1 - x) + c}
    y_dev = {'tp': 1 - y}

    def piece(half, kind, far, sub):
        return half * 8 + kind * 4 + far * 2 + sub

    order = []
    for far_x, far_y in ((1 - x, 1 - y), (x, y)):
        for half in (1 - c, c):
            for kind, far in ((0, far_x), (1, far_y)):
                for sub in ((1 - y, y) if kind == 0 else (1 - x, x)):
                    order.append(piece(half, kind, far, sub))

    copies = {}

    def start(key, src, dst, sem):
        cp = pltpu.make_async_copy(src, dst, sem)
        cp.start()
        copies[key] = cp

    rem_row = pl.multiple_of((8 * c + 4 * x) * hd, hd)
    for i in range(n_pieces):
        start(('o', i), wo_hbm.at[layer, pl.ds(rem_row, k_loc), pl.ds(pl.multiple_of(order[i] * PC, PC), PC)], wo_v.at[i], wo_sem.at[i])

    barrier = pltpu.get_barrier_semaphore()
    for dev in (core_dev, x_dev, y_dev):
        pl.semaphore_signal(barrier, inc=1, device_id=dev, device_id_type=MESH)
    pl.semaphore_wait(barrier, 3)

    def remote(src, dst, send, recv, dev):
        cp = pltpu.make_async_remote_copy(src_ref=src, dst_ref=dst, send_sem=send, recv_sem=recv, device_id=dev, device_id_type=MESH)
        cp.start()
        return cp

    hh = heads // 2
    hq = heads // 4
    sr = sm_ref.shape[0]
    away = 1 - c
    d_cp = [
        remote(sm_ref.at[pl.ds(pl.multiple_of(away * (sr // 2), 8), sr // 2)], r_st.at[0], m_send.at[0], m_recv.at[0], core_dev),
        remote(sl_ref.at[pl.ds(pl.multiple_of(away * (sr // 2), 8), sr // 2)], r_st.at[1], m_send.at[1], m_recv.at[1], core_dev),
        remote(o_ref.at[pl.ds(away * hh, hh)], r_o, m_send.at[2], m_recv.at[2], core_dev),
    ]

    f_off = pl.multiple_of(sp * f_loc, PC)
    def gate_copy(i):
        col = pl.ds(pl.multiple_of(f_off + i * PC, PC), PC)
        return (pltpu.make_async_copy(wg_hbm.at[layer, :, col], wg_v.at[i], wg_sem.at[i]),
                pltpu.make_async_copy(wu_hbm.at[layer, :, col], wu_v.at[i], wu_sem.at[i]))

    for i in range(n_f):
        for cp in gate_copy(i):
            cp.start()
    for i in range(n_pieces):
        start(('d', i), wd_hbm.at[layer, pl.ds(f_off, f_loc), pl.ds(pl.multiple_of(order[i] * PC, PC), PC)], wd_v.at[i], wd_sem.at[i])

    for cp in d_cp:
        cp.wait_recv()

    def merge_into(dst, st_dst, src_o, m1, l1, src_o2, m2, l2, n_heads):
        mx = jnp.maximum(m1, m2)
        f1 = jnp.exp(m1 - mx)
        f2 = jnp.exp(m2 - mx)
        ln = l1 * f1 + l2 * f2
        st_dst(mx, ln)
        for h in range(n_heads):
            for t in range(rows // 8):
                a = jnp.broadcast_to(f1[8 * h:8 * h + 8, t:t + 1], (8, hd))
                b = jnp.broadcast_to(f2[8 * h:8 * h + 8, t:t + 1], (8, hd))
                dst(h, t, src_o(h, t) * a + src_o2(h, t) * b, ln)

    def core_merge(q4, dst_o, slot):
        lo = pl.multiple_of(c * (sr // 2) + q4 * (sr // 4), 8)
        lr = pl.multiple_of(q4 * (sr // 4), 8)
        n = sr // 4

        def st_dst(mx, ln):
            mst[slot, 0] = mx
            mst[slot, 1] = ln

        def dst(h, t, val, ln):
            dst_o[h, 8 * t:8 * t + 8, :] = val

        merge_into(dst, st_dst,
                   lambda h, t: o_ref[c * hh + q4 * hq + h, 8 * t:8 * t + 8, :], sm_ref[pl.ds(lo, n)], sl_ref[pl.ds(lo, n)],
                   lambda h, t: r_o[q4 * hq + h, 8 * t:8 * t + 8, :], r_st[0, pl.ds(lr, n)], r_st[1, pl.ds(lr, n)], hq)

    core_merge(1 - x, mo_s, 0)
    x_cp = [
        remote(mst.at[0], r_st2, m_send.at[3], m_recv.at[3], x_dev),
        remote(mo_s, r_o2, m_send.at[4], m_recv.at[4], x_dev),
    ]
    core_merge(x, mo_k, 1)
    for cp in x_cp:
        cp.wait_recv()

    def fin(h, t, val, ln):
        den = jnp.broadcast_to(ln[8 * h:8 * h + 8, t:t + 1], (8, hd))
        mo_k[h, 8 * t:8 * t + 8, :] = val / den

    merge_into(fin, lambda mx, ln: None,
               lambda h, t: mo_k[h, 8 * t:8 * t + 8, :], mst[1, 0], mst[1, 1],
               lambda h, t: r_o2[h, 8 * t:8 * t + 8, :], r_st2[0], r_st2[1], hq)
    for h in range(hq):
        att[:, h * hd:(h + 1) * hd] = mo_k[h].astype(BF16)
    for cp in d_cp + x_cp:
        cp.wait_send()

    def all_reduce(product, resid, g):
        sends = []

        def rs(n, src, dst, dev):
            cp = remote(src, dst, rs_send.at[n], rs_recv.at[n], dev)
            sends.append(cp)
            return cp

        def core_part(first, at):
            out = []
            for k in range(2):
                for i in (first + 2 * k, first + 2 * k + 1):
                    part[i] = product(i)
                out.append(rs(at // 2 + k, part.at[pl.ds(first + 2 * k, 2)], r_d.at[pl.ds(at + 2 * k, 2)], core_dev))
            return out

        d_in = core_part(0, 0)
        link = []
        for k, (buf, dev) in enumerate(((r_x1, x_dev), (r_y1, y_dev))):
            for j in range(2):
                i = 4 + 2 * k + j
                part[i] = product(i)
                if j == 0:
                    d_in[k].wait_recv()
                part[i] = part[i] + r_d[2 * k + j]
                link.append(rs(4 + 2 * k + j, part.at[i], buf.at[j], dev))
        d_in = core_part(8, 4)
        for k in range(2):
            for j in range(2):
                i = 12 + 2 * k + j
                part[i] = product(i)
                if j == 0:
                    d_in[k].wait_recv()
                part[i] = part[i] + r_d[4 + 2 * k + j]
        link[0].wait_recv()
        part[12] = part[12] + r_x1[0]
        a2 = rs(8, part.at[12], r_y2, y_dev)
        link[2].wait_recv()
        part[14] = part[14] + r_y1[0]
        b2 = rs(9, part.at[14], r_x2, x_dev)
        link[1].wait_recv()
        part[13] = part[13] + r_x1[1]
        link[3].wait_recv()
        part[15] = part[15] + r_y1[1]

        gs = []

        def ag(n, p, dev):
            cp = remote(g.at[p], g.at[p], ag_send.at[n], ag_recv.at[n], dev)
            gs.append(cp)
            return cp

        pa = piece(c, 0, x, y)
        pb = piece(c, 1, y, x)
        a2.wait_recv()
        g[pa] = (resid(pa) + (part[13] + r_y2[...])).astype(BF16).astype(F32)
        ya = ag(0, pa, y_dev)
        b2.wait_recv()
        g[pb] = (resid(pb) + (part[15] + r_x2[...])).astype(BF16).astype(F32)
        xb = ag(3, pb, x_dev)
        xa = ag(1, pa, x_dev)
        yb = ag(4, pb, y_dev)
        d0 = ag(2, pa, core_dev)
        d1 = ag(5, pb, core_dev)
        ya.wait_recv()
        p = piece(c, 0, x, 1 - y)
        xf = ag(6, p, x_dev)
        d2 = ag(7, p, core_dev)
        xb.wait_recv()
        p = piece(c, 1, y, 1 - x)
        yf = ag(8, p, y_dev)
        d3 = ag(9, p, core_dev)
        xa.wait_recv()
        d4 = ag(10, piece(c, 0, 1 - x, y), core_dev)
        yb.wait_recv()
        d5 = ag(11, piece(c, 1, 1 - y, x), core_dev)
        xf.wait_recv()
        d6 = ag(12, piece(c, 0, 1 - x, 1 - y), core_dev)
        yf.wait_recv()
        d7 = ag(13, piece(c, 1, 1 - y, 1 - x), core_dev)
        for cp in (d0, d1, d2, d3, d4, d5, d6, d7):
            cp.wait_recv()
        for cp in sends + gs:
            cp.wait_send()

    def out_product(i):
        copies[('o', i)].wait()
        return jnp.dot(att[...], wo_v[i], preferred_element_type=F32)

    def u_resid(p):
        return u_ref[:, pl.ds(pl.multiple_of(p * PC, PC), PC)].astype(F32)

    all_reduce(out_product, u_resid, g1)

    def norm(g, gains, row):
        sq = jnp.zeros((rows, PC), F32)
        for i in range(n_pieces):
            sq = sq + g[i] * g[i]
        inv = lax.rsqrt(jnp.sum(sq, axis=-1, keepdims=True) * (1.0 / d_model) + EPS)
        for i in range(n_pieces):
            cols = slice(i * PC, (i + 1) * PC)
            h2[:, cols] = (g[i] * inv * gains[row:row + 1, cols].astype(F32)).astype(BF16)

    norm(g1, gain_ref, layer)

    def gate_up(i, _):
        cg, cu = gate_copy(i)
        cg.wait()
        ga = jnp.dot(h2[...], wg_v[i], preferred_element_type=F32)
        cu.wait()
        up = jnp.dot(h2[...], wu_v[i], preferred_element_type=F32)
        act[:, pl.ds(pl.multiple_of(i * PC, PC), PC)] = (ga * jax.nn.sigmoid(ga) * up).astype(BF16)
        return 0

    lax.fori_loop(0, n_f, gate_up, 0)

    n_q = q_ref.shape[0] * hd // (2 * PC) if has_next else 0

    def next_copy(j):
        out = []
        for t, (buf, sem) in enumerate(((wg_v, wg_sem), (wu_v, wu_sem))):
            if isinstance(j, int) and j >= n_q:
                src = (wk_hbm, wv_hbm)[j - n_q].at[layer + 1, :, t * PC:(t + 1) * PC]
            else:
                src = wq_hbm.at[layer + 1, :, pl.ds(pl.multiple_of((2 * j + t) * PC, PC), PC)]
            out.append(pltpu.make_async_copy(src, buf.at[j], sem.at[j]))
        return out

    if has_next:
        for j in range(n_q + 2):
            for cp in next_copy(j):
                cp.start()

    def down_product(i):
        copies[('d', i)].wait()
        return jnp.dot(act[...], wd_v[i], preferred_element_type=F32)

    all_reduce(down_product, lambda p: g1[p], g2)
    back = permutation(rows, n_steps, False) if last else None
    for i in range(n_pieces):
        val = g2[i].astype(BF16)
        if last:
            val = jnp.dot(back, val, preferred_element_type=F32).astype(BF16)
        out_ref[:, i * PC:(i + 1) * PC] = val

    if has_next:
        norm(g2, gain_a_ref, layer + 1)
        cos_a, sin_a = cos_ref[...], sin_ref[...]

        def rot(z):
            return (z * cos_a + pltpu.roll(z, hd // 2, 1) * sin_a).astype(BF16).astype(F32)

        def heads_of(j, store):
            for t, (buf, cp) in enumerate(zip((wg_v, wu_v), next_copy(j))):
                cp.wait()
                val = jnp.dot(h2[...], buf[j], preferred_element_type=F32)
                for e in range(PC // hd):
                    store(t * (PC // hd) + e, val[:, e * hd:(e + 1) * hd])

        def q_pair(j, _):
            def store(e, val):
                q_ref[2 * (PC // hd) * j + e] = rot(val)
            heads_of(j, store)
            return 0

        def store_k(e, val):
            k_ref[e] = rot(val)

        def store_v(e, val):
            v_ref[e] = val.astype(BF16).astype(F32)

        lax.fori_loop(0, n_q, q_pair, 0)
        heads_of(n_q, store_k)
        heads_of(n_q + 1, store_v)


def block_call(layer, last, n_steps, o, sm, sl, u, gain, wo, wg, wu, wd, sp_size, nxt):
    rows, d_model = u.shape
    heads, _, hd = o.shape
    n_p = d_model // PC
    k_loc = wo.shape[1] // sp_size
    f_loc = wd.shape[1] // sp_size
    n_f = f_loc // PC
    sr = sm.shape[0]
    V = pltpu.VMEM
    dma = pltpu.SemaphoreType.DMA
    vm = pl.BlockSpec(memory_space=pltpu.VMEM)
    hbm = pl.BlockSpec(memory_space=pl.ANY)
    return pl.pallas_call(
        functools.partial(block_kernel, layer, last, n_steps),
        out_shape=[jax.ShapeDtypeStruct((rows, d_model), BF16)] + ([] if last else [
            jax.ShapeDtypeStruct((heads, rows, hd), F32),
            jax.ShapeDtypeStruct((nxt[4].shape[2] // hd, rows, hd), F32),
            jax.ShapeDtypeStruct((nxt[4].shape[2] // hd, rows, hd), F32)]),
        in_specs=[vm] * 5 + [hbm] * 4 + ([] if last else [vm] * 3 + [hbm] * 3),
        out_specs=[vm] * (1 if last else 4),
        scratch_shapes=[
            V((n_p, k_loc, PC), BF16), V((n_f, d_model, PC), BF16), V((n_f, d_model, PC), BF16), V((n_p, f_loc, PC), BF16),
            V((n_p, rows, PC), F32), V((n_p, rows, PC), F32), V((n_p, rows, PC), F32),
            V((rows, d_model), BF16), V((rows, f_loc), BF16), V((rows, k_loc), BF16),
            V((n_p // 2, rows, PC), F32), V((2, rows, PC), F32), V((2, rows, PC), F32), V((rows, PC), F32), V((rows, PC), F32),
            V((heads // 2, rows, hd), F32), V((2, sr // 2, 128), F32),
            V((heads // 4, rows, hd), F32), V((heads // 4, rows, hd), F32), V((2, 2, sr // 4, 128), F32),
            V((heads // 4, rows, hd), F32), V((2, sr // 4, 128), F32),
            dma((n_p,)), dma((n_f,)), dma((n_f,)), dma((n_p,)),
            dma((5,)), dma((5,)), dma((10,)), dma((10,)), dma((14,)), dma((14,)),
        ],
        compiler_params=pltpu.CompilerParams(collective_id=layer, has_side_effects=True, vmem_limit_bytes=VMEM_ALL),
        name=f'block{layer}',
    )(o, sm, sl, u, gain, wo, wg, wu, wd, *nxt)


def solution(mesh):
    sp_size = mesh.shape['sp']

    def local_fn(tok_emb, lengths, key_cache, val_cache, gain_attn, gain_mlp, w_query, w_key, w_value, w_out, w_gate, w_up, w_down):
        n_steps, n_batch, d_model = tok_emb.shape
        n_layers, _, loc_len, kv_loc, hd = key_cache.shape
        rows = n_steps * n_batch
        first_pos = loc_len * sp_size // 2
        table = jnp.asarray(rope_table(first_pos, first_pos, hd))
        u = tok_emb.reshape(rows, d_model)
        kc = key_cache.reshape(n_layers, n_batch, loc_len * kv_loc, hd)
        vc = val_cache.reshape(n_layers, n_batch, loc_len * kv_loc, hd)
        prev = None
        for layer in range(n_layers):
            last = layer == n_layers - 1
            if layer == 0:
                q, k, v, cos_a, sin_a, u = qkv_call(layer, u, gain_attn, table, lengths, w_query, w_key, w_value, n_steps, hd, first_pos)
            nk, nv, o, sm, sl = attn_call(layer, lengths, q, k, v, kc, vc, prev, kv_loc, n_steps, sp_size)
            prev = (nk, nv)
            nxt = () if last else (gain_attn, cos_a, sin_a, w_query, w_key, w_value)
            outs = block_call(layer, last, n_steps, o, sm, sl, u, gain_mlp, w_out, w_gate, w_up, w_down, sp_size, nxt)
            u = outs[0]
            if not last:
                q, k, v = outs[1:]
        return u.reshape(n_steps, n_batch, d_model), prev[0].reshape(key_cache.shape), prev[1].reshape(val_cache.shape)

    cache_spec = P(None, 'dp', 'sp', 'tp', None)
    col_spec = P(None, None, 'tp')
    row_spec = P(None, 'tp', None)
    emb_spec = P(None, 'dp', None)
    return jax.shard_map(local_fn, mesh=mesh, in_specs=(emb_spec, P('dp'), cache_spec, cache_spec, P(), P(), col_spec, col_spec, col_spec, row_spec, col_spec, col_spec, row_spec), out_specs=(emb_spec, cache_spec, cache_spec), check_vma=False)
```

time: 251 us -> 206 us (0.82)
  Pallas kernels: 226 us -> 202 us
  local copies, waits for them, and re-layouts: 16.3 us -> 2.29 us
  other arithmetic: 6.08 us -> 0 us
    pallas_call x6 -> x5, Pallas kernels: 226 us -> 202 us  [the longest x2 160 us: block_call(): pl.pallas_call(functools.partial(block_kernel, layer, last, n_steps), out...]
    unnamed x24 -> x1, local copies, waits for them, and re-layouts: 6.94 us -> 2.29 us
    reshape x3 -> x0, local copies, waits for them, and re-layouts: 4.12 us -> none  [the longest x2 3.01 us: local_fn(): hidden = u.reshape(n_batch, n_steps, d_model).transpose(1, 0, 2)]
    slice x2 -> x0, local copies, waits for them, and re-layouts: 2.87 us -> none  [the longest x1 1.44 us: local_fn(): gain_attn[layer][None]]
    reduce_sum x2 -> x0, other arithmetic: 2.81 us -> none  [own_row(): t = jnp.sum(jnp.where(mine[None, :, :, None], t, jnp.zeros_like(t)), axis=2)]
where the time goes in v3:
time: 206 us; the launch traced here: 205 us
  Pallas kernels  202 us (98%)
  local copies, waits for them, and re-layouts  2.29 us (1%)
    pallas_call x2, Pallas kernels, block_call(): pl.pallas_call(functools.partial(block_kernel, layer, last, n_steps), out...  160 us
    pallas_call x2, Pallas kernels, attn_call(): pl.pallas_call(functools.partial(attn_kernel, layer, n_kv, n_steps, sp_si...  29.1 us
    pallas_call x1, Pallas kernels, qkv_call(): pl.pallas_call(functools.partial(qkv_kernel, layer, n_steps, first_pos, f...  13.1 us

profile of v3, /device:TPU:0, one launch (start us, length us, event | category | flops | bytes accessed | tf_op | source)
XLA Modules:
  0.0 205.4 jit_solution(931731226232691554)
XLA Ops:
  0.6 13.1 %qkv0.1 = (f32[16,128,128]{2,1,0:T(8,128)}, f32[4,128,128]{2,1,0:T(8,128)}, f32[4,128,128]{2,1,0:T(8,128)}, f32[128,128]{1,0:T(8,128)}, f32[128,128]{1,0:T(8,128)}, /*index=5*/bf16[128,4096]{1,0:T(8,128)(2,1)}) custom-call(s32[32]{0:T(128)} %len_ref.3, f32[512,128]{1,0:T(8,128)} %constant.2.clone.refs_1_, bf16[128,4096]{1,0:T(8,128)(2,1)} %bitcast.13, ...), custom_call_target="tpu_custom_call" | custom-call | tf_op jit(solution)/shard_map/qkv0/pallas_call | solution.py:111
  13.7 14.6 %attn0.1 = (bf16[2,32,1024,128]{3,2,1,0:T(8,128)(2,1)}, bf16[2,32,1024,128]{3,2,1,0:T(8,128)(2,1)}, f32[16,128,128]{2,1,0:T(8,128)}, f32[128,128]{1,0:T(8,128)}, f32[128,128]{1,0:T(8,128)}) custom-call(s32[32]{0:T(128)} %len_ref.3, f32[16,128,128]{2,1,0:T(8,128)} %get-tuple-element.23.q_ref, f32[4,128,128]{2,1,0:T(8,128)} %get-tuple-element.24.kn_ref, ...), custom_call_target="tpu_custom_call" | custom-call | tf_op jit(solution)/shard_map/attn0/pallas_call | solution.py:242
  28.3 85.8 %block0.1 = (bf16[128,4096]{1,0:T(8,128)(2,1)}, f32[16,128,128]{2,1,0:T(8,128)}, f32[4,128,128]{2,1,0:T(8,128)}, f32[4,128,128]{2,1,0:T(8,128)}) custom-call(f32[16,128,128]{2,1,0:T(8,128)} %get-tuple-element.26.o_ref, f32[128,128]{1,0:T(8,128)} %get-tuple-element.27.sm_ref, f32[128,128]{1,0:T(8,128)} %get-tuple-element.28.sl_ref, ...), custom_call_target="tpu_custom_call" | custom-call | tf_op jit(solution)/shard_map/block0/pallas_call | solution.py:589
  114.1 14.5 %attn1.1 = (bf16[2,32,1024,128]{3,2,1,0:T(8,128)(2,1)}, bf16[2,32,1024,128]{3,2,1,0:T(8,128)(2,1)}, f32[16,128,128]{2,1,0:T(8,128)}, f32[128,128]{1,0:T(8,128)}, f32[128,128]{1,0:T(8,128)}) custom-call(s32[32]{0:T(128)} %len_ref.3, f32[16,128,128]{2,1,0:T(8,128)} %get-tuple-element.32.q_ref, ...), custom_call_target="tpu_custom_call", output_to_operand_aliasing={{0}: (6, {}), {1}: (7, {})} | custom-call | tf_op jit(solution)/shard_map/attn1/pallas_call | solution.py:242
  128.6 74.4 %block1.1 = bf16[128,4096]{1,0:T(8,128)(2,1)} custom-call(f32[16,128,128]{2,1,0:T(8,128)} %get-tuple-element.37.o_ref, f32[128,128]{1,0:T(8,128)} %get-tuple-element.38.sm_ref, f32[128,128]{1,0:T(8,128)} %get-tuple-element.39.sl_ref, bf16[128,4096]{1,0:T(8,128)(2,1)} %get-tuple-element.40.u_ref, bf16[2,4096]{1,0:T(2,128)(2,1)} %gain_ref.3, ...), custom_call_target="tpu_custom_call" | custom-call | tf_op jit(solution)/shard_map/block1/pallas_call | solution.py:589
  203.1 2.3 %copy.22 = bf16[4,32,4096]{2,1,0:T(8,128)(2,1)} copy(bf16[4,32,4096]{2,1,0:T(8,128)(2,1)} %bitcast.12) | data formatting | bytes 2097152

commit v4 on v3

--- a/solution.py
+++ b/solution.py
@@ -121,8 +121,8 @@
 
 
 SEQS = 4
-SLOTS = 6
-AHEAD = 4
+SLOTS = 8
+AHEAD = 8
 
 
 def attn_kernel(layer, n_kv, n_steps, sp_size, has_prev, len_ref, q_ref, kn_ref, vn_ref, k_hbm, v_hbm, *rest):
@@ -150,7 +150,7 @@
         return (pltpu.make_async_copy(kb.at[slot], ko_hbm.at[layer, dst], out_sem.at[slot, 0]),
                 pltpu.make_async_copy(vb.at[slot], vo_hbm.at[layer, dst], out_sem.at[slot, 1]))
 
-    for i in range(AHEAD):
+    for i in range(min(AHEAD, n_iter)):
         for cp in reads(i):
             cp.start()
 
@@ -209,19 +209,20 @@
         sm_ref[...] = sm
         sl_ref[...] = sl
 
-        @pl.when(i + AHEAD >= SLOTS)
-        def _():
-            for cp in writes(i + AHEAD - SLOTS):
-                cp.wait()
-
-        @pl.when(i + AHEAD < n_iter)
-        def _():
-            for cp in reads(i + AHEAD):
-                cp.start()
+        if AHEAD < n_iter:
+            @pl.when(jnp.logical_and(i + AHEAD >= SLOTS, i + AHEAD < n_iter))
+            def _():
+                for cp in writes(i + AHEAD - SLOTS):
+                    cp.wait()
+
+            @pl.when(i + AHEAD < n_iter)
+            def _():
+                for cp in reads(i + AHEAD):
+                    cp.start()
         return 0
 
     lax.fori_loop(0, n_iter, body, 0)
-    for i in range(n_iter + AHEAD - SLOTS, n_iter):
+    for i in range(max(0, n_iter - SLOTS), n_iter):
         for cp in writes(i):
             cp.wait()
 
@@ -259,19 +260,19 @@
     )(*args)
 
 
-def block_kernel(layer, last, n_steps, o_ref, sm_ref, sl_ref, u_ref, gain_ref, wo_hbm, wg_hbm, wu_hbm, wd_hbm, *refs):
+def block_kernel(layer, last, n_steps, o_hbm, sm_hbm, sl_hbm, u_hbm, gain_ref, wo_hbm, wg_hbm, wu_hbm, wd_hbm, *refs):
     has_next = not last
     if has_next:
         gain_a_ref, cos_ref, sin_ref, wq_hbm, wk_hbm, wv_hbm, out_ref, q_ref, k_ref, v_ref, *refs = refs
     else:
         out_ref, *refs = refs
-    block_body(layer, last, n_steps, has_next, o_ref, sm_ref, sl_ref, u_ref, gain_ref, wo_hbm, wg_hbm, wu_hbm, wd_hbm,
+    block_body(layer, last, n_steps, has_next, o_hbm, sm_hbm, sl_hbm, u_hbm, gain_ref, wo_hbm, wg_hbm, wu_hbm, wd_hbm,
                (gain_a_ref, cos_ref, sin_ref, wq_hbm, wk_hbm, wv_hbm) if has_next else None, out_ref,
                (q_ref, k_ref, v_ref) if has_next else None, *refs)
 
 
-def block_body(layer, last, n_steps, has_next, o_ref, sm_ref, sl_ref, u_ref, gain_ref, wo_hbm, wg_hbm, wu_hbm, wd_hbm, nxt, out_ref, qkv,
-                 wo_v, wg_v, wu_v, wd_v, part, g1, g2, h2, act, att,
+def block_body(layer, last, n_steps, has_next, o_hbm, sm_hbm, sl_hbm, u_hbm, gain_ref, wo_hbm, wg_hbm, wu_hbm, wd_hbm, nxt, out_ref, qkv,
+                 o_ref, sm_ref, sl_ref, u_ref, in_sem, wo_v, wg_v, wu_v, wd_v, part, g1, g2, h2, act, att,
                  r_d, r_x1, r_y1, r_x2, r_y2, r_o, r_st, mo_s, mo_k, mst, r_o2, r_st2,
                  wo_sem, wg_sem, wu_sem, wd_sem, m_send, m_recv, rs_send, rs_recv, ag_send, ag_recv):
     if has_next:
@@ -303,6 +304,14 @@
                 for sub in ((1 - y, y) if kind == 0 else (1 - x, x)):
                     order.append(piece(half, kind, far, sub))
 
+    in_copies = {}
+    half_rows = rows // 2
+    half_of = [pl.ds(r * half_rows, half_rows) for r in range(2)]
+    for n, (key, src, dst) in enumerate((
+            ('m', sm_hbm, sm_ref), ('l', sl_hbm, sl_ref), (0, o_hbm.at[:, half_of[0]], o_ref.at[:, half_of[0]]),
+            (1, o_hbm.at[:, half_of[1]], o_ref.at[:, half_of[1]]), ('u', u_hbm, u_ref))):
+        in_copies[key] = pltpu.make_async_copy(src, dst, in_sem.at[n])
+        in_copies[key].start()
     copies = {}
 
     def start(key, src, dst, sem):
@@ -312,7 +321,8 @@
 
     rem_row = pl.multiple_of((8 * c + 4 * x) * hd, hd)
     for i in range(n_pieces):
-        start(('o', i), wo_hbm.at[layer, pl.ds(rem_row, k_loc), pl.ds(pl.multiple_of(order[i] * PC, PC), PC)], wo_v.at[i], wo_sem.at[i])
+        start(('o', i), wo_hbm.at[layer, pl.ds(rem_row, k_loc), pl.ds(pl.multiple_of(order[i] * PC, PC), PC)],
+              wo_v.at[i // 2, :, (i % 2) * PC:(i % 2 + 1) * PC], wo_sem.at[i])
 
     barrier = pltpu.get_barrier_semaphore()
     for dev in (core_dev, x_dev, y_dev):
@@ -328,11 +338,16 @@
     hq = heads // 4
     sr = sm_ref.shape[0]
     away = 1 - c
-    d_cp = [
-        remote(sm_ref.at[pl.ds(pl.multiple_of(away * (sr // 2), 8), sr // 2)], r_st.at[0], m_send.at[0], m_recv.at[0], core_dev),
-        remote(sl_ref.at[pl.ds(pl.multiple_of(away * (sr // 2), 8), sr // 2)], r_st.at[1], m_send.at[1], m_recv.at[1], core_dev),
-        remote(o_ref.at[pl.ds(away * hh, hh)], r_o, m_send.at[2], m_recv.at[2], core_dev),
-    ]
+    away_rows = pl.ds(pl.multiple_of(away * (sr // 2), 8), sr // 2)
+    in_copies['m'].wait()
+    in_copies['l'].wait()
+    d_st = [remote(sm_ref.at[away_rows], r_st.at[0], m_send.at[0], m_recv.at[0], core_dev),
+            remote(sl_ref.at[away_rows], r_st.at[1], m_send.at[1], m_recv.at[1], core_dev)]
+    d_o = []
+    for r in range(2):
+        in_copies[r].wait()
+        d_o.append(remote(o_ref.at[pl.ds(away * hh, hh), half_of[r]], r_o.at[:, half_of[r]], m_send.at[2 + r], m_recv.at[2 + r], core_dev))
+    pending = d_st + d_o
 
     f_off = pl.multiple_of(sp * f_loc, PC)
     def gate_copy(i):
@@ -344,153 +359,185 @@
         for cp in gate_copy(i):
             cp.start()
     for i in range(n_pieces):
-        start(('d', i), wd_hbm.at[layer, pl.ds(f_off, f_loc), pl.ds(pl.multiple_of(order[i] * PC, PC), PC)], wd_v.at[i], wd_sem.at[i])
-
-    for cp in d_cp:
-        cp.wait_recv()
-
-    def merge_into(dst, st_dst, src_o, m1, l1, src_o2, m2, l2, n_heads):
+        start(('d', i), wd_hbm.at[layer, pl.ds(f_off, f_loc), pl.ds(pl.multiple_of(order[i] * PC, PC), PC)],
+              wd_v.at[i // 2, :, (i % 2) * PC:(i % 2 + 1) * PC], wd_sem.at[i])
+
+    def merge_into(r, dst, st_dst, src_o, m1, l1, src_o2, m2, l2, n_heads):
         mx = jnp.maximum(m1, m2)
         f1 = jnp.exp(m1 - mx)
         f2 = jnp.exp(m2 - mx)
         ln = l1 * f1 + l2 * f2
         st_dst(mx, ln)
         for h in range(n_heads):
-            for t in range(rows // 8):
+            for t in range(r * half_rows // 8, (r + 1) * half_rows // 8):
                 a = jnp.broadcast_to(f1[8 * h:8 * h + 8, t:t + 1], (8, hd))
                 b = jnp.broadcast_to(f2[8 * h:8 * h + 8, t:t + 1], (8, hd))
                 dst(h, t, src_o(h, t) * a + src_o2(h, t) * b, ln)
 
-    def core_merge(q4, dst_o, slot):
+    def core_merge(r, q4, dst_o, slot):
         lo = pl.multiple_of(c * (sr // 2) + q4 * (sr // 4), 8)
         lr = pl.multiple_of(q4 * (sr // 4), 8)
         n = sr // 4
 
         def st_dst(mx, ln):
-            mst[slot, 0] = mx
-            mst[slot, 1] = ln
+            if r == 0:
+                mst[slot, 0] = mx
+                mst[slot, 1] = ln
 
         def dst(h, t, val, ln):
             dst_o[h, 8 * t:8 * t + 8, :] = val
 
-        merge_into(dst, st_dst,
+        merge_into(r, dst, st_dst,
                    lambda h, t: o_ref[c * hh + q4 * hq + h, 8 * t:8 * t + 8, :], sm_ref[pl.ds(lo, n)], sl_ref[pl.ds(lo, n)],
                    lambda h, t: r_o[q4 * hq + h, 8 * t:8 * t + 8, :], r_st[0, pl.ds(lr, n)], r_st[1, pl.ds(lr, n)], hq)
 
-    core_merge(1 - x, mo_s, 0)
-    x_cp = [
-        remote(mst.at[0], r_st2, m_send.at[3], m_recv.at[3], x_dev),
-        remote(mo_s, r_o2, m_send.at[4], m_recv.at[4], x_dev),
-    ]
-    core_merge(x, mo_k, 1)
-    for cp in x_cp:
-        cp.wait_recv()
-
-    def fin(h, t, val, ln):
-        den = jnp.broadcast_to(ln[8 * h:8 * h + 8, t:t + 1], (8, hd))
-        mo_k[h, 8 * t:8 * t + 8, :] = val / den
-
-    merge_into(fin, lambda mx, ln: None,
-               lambda h, t: mo_k[h, 8 * t:8 * t + 8, :], mst[1, 0], mst[1, 1],
-               lambda h, t: r_o2[h, 8 * t:8 * t + 8, :], r_st2[0], r_st2[1], hq)
-    for h in range(hq):
-        att[:, h * hd:(h + 1) * hd] = mo_k[h].astype(BF16)
-    for cp in d_cp + x_cp:
-        cp.wait_send()
-
-    def all_reduce(product, resid, g):
-        sends = []
-
-        def rs(n, src, dst, dev):
-            cp = remote(src, dst, rs_send.at[n], rs_recv.at[n], dev)
-            sends.append(cp)
-            return cp
+    x_st = []
+
+    def merge_chain(r):
+        if r == 0:
+            for cp in d_st:
+                cp.wait_recv()
+        d_o[r].wait_recv()
+        core_merge(r, 1 - x, mo_s, 0)
+        if r == 0:
+            x_st.append(remote(mst.at[0], r_st2, m_send.at[4], m_recv.at[4], x_dev))
+            pending.append(x_st[0])
+        x_o = remote(mo_s.at[:, half_of[r]], r_o2.at[:, half_of[r]], m_send.at[5 + r], m_recv.at[5 + r], x_dev)
+        pending.append(x_o)
+        core_merge(r, x, mo_k, 1)
+        yield
+        if r == 0:
+            x_st[0].wait_recv()
+        x_o.wait_recv()
+
+        def fin(h, t, val, ln):
+            den = jnp.broadcast_to(ln[8 * h:8 * h + 8, t:t + 1], (8, hd))
+            mo_k[h, 8 * t:8 * t + 8, :] = val / den
+
+        merge_into(r, fin, lambda mx, ln: None,
+                   lambda h, t: mo_k[h, 8 * t:8 * t + 8, :], mst[1, 0], mst[1, 1],
+                   lambda h, t: r_o2[h, 8 * t:8 * t + 8, :], r_st2[0], r_st2[1], hq)
+        for h in range(hq):
+            att[half_of[r], h * hd:(h + 1) * hd] = mo_k[h, half_of[r]].astype(BF16)
+
+    def rs(r, n, src, dst, dev):
+        cp = remote(src, dst, rs_send.at[10 * r + n], rs_recv.at[10 * r + n], dev)
+        pending.append(cp)
+        return cp
+
+    def sum_front(halves, product):
+        r0 = halves[0]
+        R = pl.ds(r0 * half_rows, len(halves) * half_rows)
+        link = {r: [None] * 4 for r in halves}
 
         def core_part(first, at):
             out = []
             for k in range(2):
-                for i in (first + 2 * k, first + 2 * k + 1):
-                    part[i] = product(i)
-                out.append(rs(at // 2 + k, part.at[pl.ds(first + 2 * k, 2)], r_d.at[pl.ds(at + 2 * k, 2)], core_dev))
+                i = first + 2 * k
+                val = product(i // 2, R, r0 == 0)
+                part[i, R] = val[:, :PC]
+                part[i + 1, R] = val[:, PC:]
+                out.append(rs(r0, at // 2 + k, part.at[pl.ds(i, 2), R], r_d.at[pl.ds(at + 2 * k, 2), R], core_dev))
             return out
 
+        def own_part(first, at, k, d_in):
+            i = first + 2 * k
+            val = product(i // 2, R, r0 == 0)
+            d_in[k].wait_recv()
+            part[i, R] = val[:, :PC] + r_d[at + 2 * k, R]
+            part[i + 1, R] = val[:, PC:] + r_d[at + 2 * k + 1, R]
+
         d_in = core_part(0, 0)
-        link = []
         for k, (buf, dev) in enumerate(((r_x1, x_dev), (r_y1, y_dev))):
-            for j in range(2):
-                i = 4 + 2 * k + j
-                part[i] = product(i)
-                if j == 0:
-                    d_in[k].wait_recv()
-                part[i] = part[i] + r_d[2 * k + j]
-                link.append(rs(4 + 2 * k + j, part.at[i], buf.at[j], dev))
+            own_part(4, 0, k, d_in)
+            for r in halves:
+                for j in range(2):
+                    link[r][2 * k + j] = rs(r, 4 + 2 * k + j, part.at[4 + 2 * k + j, half_of[r]], buf.at[j, half_of[r]], dev)
         d_in = core_part(8, 4)
         for k in range(2):
-            for j in range(2):
-                i = 12 + 2 * k + j
-                part[i] = product(i)
-                if j == 0:
-                    d_in[k].wait_recv()
-                part[i] = part[i] + r_d[4 + 2 * k + j]
+            own_part(12, 4, k, d_in)
+        return link
+
+    def sum_back(r, link, resid, g):
+        R = half_of[r]
+
+        def ag(n, p, dev):
+            cp = remote(g.at[p, R], g.at[p, R], ag_send.at[14 * r + n], ag_recv.at[14 * r + n], dev)
+            pending.append(cp)
+            return cp
+
         link[0].wait_recv()
-        part[12] = part[12] + r_x1[0]
-        a2 = rs(8, part.at[12], r_y2, y_dev)
+        part[12, R] = part[12, R] + r_x1[0, R]
+        a2 = rs(r, 8, part.at[12, R], r_y2.at[R], y_dev)
         link[2].wait_recv()
-        part[14] = part[14] + r_y1[0]
-        b2 = rs(9, part.at[14], r_x2, x_dev)
+        part[14, R] = part[14, R] + r_y1[0, R]
+        b2 = rs(r, 9, part.at[14, R], r_x2.at[R], x_dev)
         link[1].wait_recv()
-        part[13] = part[13] + r_x1[1]
+        part[13, R] = part[13, R] + r_x1[1, R]
         link[3].wait_recv()
-        part[15] = part[15] + r_y1[1]
-
-        gs = []
-
-        def ag(n, p, dev):
-            cp = remote(g.at[p], g.at[p], ag_send.at[n], ag_recv.at[n], dev)
-            gs.append(cp)
-            return cp
-
+        part[15, R] = part[15, R] + r_y1[1, R]
+        yield
         pa = piece(c, 0, x, y)
         pb = piece(c, 1, y, x)
         a2.wait_recv()
-        g[pa] = (resid(pa) + (part[13] + r_y2[...])).astype(BF16).astype(F32)
+        g[pa, R] = (resid(pa, R) + (part[13, R] + r_y2[R])).astype(BF16).astype(F32)
         ya = ag(0, pa, y_dev)
         b2.wait_recv()
-        g[pb] = (resid(pb) + (part[15] + r_x2[...])).astype(BF16).astype(F32)
+        g[pb, R] = (resid(pb, R) + (part[15, R] + r_x2[R])).astype(BF16).astype(F32)
         xb = ag(3, pb, x_dev)
         xa = ag(1, pa, x_dev)
         yb = ag(4, pb, y_dev)
-        d0 = ag(2, pa, core_dev)
-        d1 = ag(5, pb, core_dev)
+        last_in = [ag(2, pa, core_dev), ag(5, pb, core_dev)]
+        yield
         ya.wait_recv()
         p = piece(c, 0, x, 1 - y)
         xf = ag(6, p, x_dev)
-        d2 = ag(7, p, core_dev)
+        last_in.append(ag(7, p, core_dev))
         xb.wait_recv()
         p = piece(c, 1, y, 1 - x)
         yf = ag(8, p, y_dev)
-        d3 = ag(9, p, core_dev)
+        last_in.append(ag(9, p, core_dev))
+        yield
         xa.wait_recv()
-        d4 = ag(10, piece(c, 0, 1 - x, y), core_dev)
+        last_in.append(ag(10, piece(c, 0, 1 - x, y), core_dev))
         yb.wait_recv()
-        d5 = ag(11, piece(c, 1, 1 - y, x), core_dev)
+        last_in.append(ag(11, piece(c, 1, 1 - y, x), core_dev))
         xf.wait_recv()
-        d6 = ag(12, piece(c, 0, 1 - x, 1 - y), core_dev)
+        last_in.append(ag(12, piece(c, 0, 1 - x, 1 - y), core_dev))
         yf.wait_recv()
-        d7 = ag(13, piece(c, 1, 1 - y, 1 - x), core_dev)
-        for cp in (d0, d1, d2, d3, d4, d5, d6, d7):
+        last_in.append(ag(13, piece(c, 1, 1 - y, 1 - x), core_dev))
+        yield
+        for cp in last_in:
             cp.wait_recv()
-        for cp in sends + gs:
+
+    def interleave(chains):
+        chains = list(chains)
+        while chains:
+            for ch in list(chains):
+                if next(ch, 'end') == 'end':
+                    chains.remove(ch)
+        for cp in pending:
             cp.wait_send()
-
-    def out_product(i):
-        copies[('o', i)].wait()
-        return jnp.dot(att[...], wo_v[i], preferred_element_type=F32)
-
-    def u_resid(p):
-        return u_ref[:, pl.ds(pl.multiple_of(p * PC, PC), PC)].astype(F32)
-
-    all_reduce(out_product, u_resid, g1)
+        pending.clear()
+
+    def out_product(k, R, fetch):
+        if fetch:
+            copies[('o', 2 * k)].wait()
+            copies[('o', 2 * k + 1)].wait()
+        return jnp.dot(att[R], wo_v[k], preferred_element_type=F32)
+
+    def u_resid(p, R):
+        return u_ref[R, pl.ds(pl.multiple_of(p * PC, PC), PC)].astype(F32)
+
+    def first_part(r):
+        yield from merge_chain(r)
+        link = sum_front([r], out_product)
+        yield
+        if r == 0:
+            in_copies['u'].wait()
+        yield from sum_back(r, link[r], u_resid, g1)
+
+    interleave(first_part(r) for r in range(2))
 
     def norm(g, gains, row):
         sq = jnp.zeros((rows, PC), F32)
@@ -531,11 +578,13 @@
             for cp in next_copy(j):
                 cp.start()
 
-    def down_product(i):
-        copies[('d', i)].wait()
-        return jnp.dot(act[...], wd_v[i], preferred_element_type=F32)
-
-    all_reduce(down_product, lambda p: g1[p], g2)
+    def down_product(k, R, fetch):
+        copies[('d', 2 * k)].wait()
+        copies[('d', 2 * k + 1)].wait()
+        return jnp.dot(act[...], wd_v[k], preferred_element_type=F32)
+
+    links = sum_front([0, 1], down_product)
+    interleave(sum_back(r, links[r], lambda p, R: g1[p, R], g2) for r in range(2))
     back = permutation(rows, n_steps, False) if last else None
     for i in range(n_pieces):
         val = g2[i].astype(BF16)
@@ -592,10 +641,11 @@
             jax.ShapeDtypeStruct((heads, rows, hd), F32),
             jax.ShapeDtypeStruct((nxt[4].shape[2] // hd, rows, hd), F32),
             jax.ShapeDtypeStruct((nxt[4].shape[2] // hd, rows, hd), F32)]),
-        in_specs=[vm] * 5 + [hbm] * 4 + ([] if last else [vm] * 3 + [hbm] * 3),
+        in_specs=[hbm] * 4 + [vm] + [hbm] * 4 + ([] if last else [vm] * 3 + [hbm] * 3),
         out_specs=[vm] * (1 if last else 4),
         scratch_shapes=[
-            V((n_p, k_loc, PC), BF16), V((n_f, d_model, PC), BF16), V((n_f, d_model, PC), BF16), V((n_p, f_loc, PC), BF16),
+            V(o.shape, F32), V(sm.shape, F32), V(sl.shape, F32), V(u.shape, BF16), dma((5,)),
+            V((n_p // 2, k_loc, 2 * PC), BF16), V((n_f, d_model, PC), BF16), V((n_f, d_model, PC), BF16), V((n_p // 2, f_loc, 2 * PC), BF16),
             V((n_p, rows, PC), F32), V((n_p, rows, PC), F32), V((n_p, rows, PC), F32),
             V((rows, d_model), BF16), V((rows, f_loc), BF16), V((rows, k_loc), BF16),
             V((n_p // 2, rows, PC), F32), V((2, rows, PC), F32), V((2, rows, PC), F32), V((rows, PC), F32), V((rows, PC), F32),
@@ -603,7 +653,7 @@
             V((heads // 4, rows, hd), F32), V((heads // 4, rows, hd), F32), V((2, 2, sr // 4, 128), F32),
             V((heads // 4, rows, hd), F32), V((2, sr // 4, 128), F32),
             dma((n_p,)), dma((n_f,)), dma((n_f,)), dma((n_p,)),
-            dma((5,)), dma((5,)), dma((10,)), dma((10,)), dma((14,)), dma((14,)),
+            dma((7,)), dma((7,)), dma((20,)), dma((20,)), dma((28,)), dma((28,)),
         ],
         compiler_params=pltpu.CompilerParams(collective_id=layer, has_side_effects=True, vmem_limit_bytes=VMEM_ALL),
         name=f'block{layer}',

time: 206 us -> 195 us (0.947)
  Pallas kernels: 202 us -> 191 us
    pallas_call x2, Pallas kernels: 160 us -> 150 us  [block_call(): pl.pallas_call(functools.partial(block_kernel, layer, last, n_steps), out...]
where the time goes in v4:
time: 195 us; the launch traced here: 194 us
  Pallas kernels  191 us (98%)
  local copies, waits for them, and re-layouts  2.29 us (1%)
    pallas_call x2, Pallas kernels, block_call(): pl.pallas_call(functools.partial(block_kernel, layer, last, n_steps), out...  150 us
    pallas_call x2, Pallas kernels, attn_call(): pl.pallas_call(functools.partial(attn_kernel, layer, n_kv, n_steps, sp_si...  28.6 us
    pallas_call x1, Pallas kernels, qkv_call(): pl.pallas_call(functools.partial(qkv_kernel, layer, n_steps, first_pos, f...  13.1 us

profile of v4, /device:TPU:0, one launch (start us, length us, event | category | flops | bytes accessed | tf_op | source)
XLA Modules:
  0.0 194.4 jit_solution(13515341027845428127)
XLA Ops:
  0.6 13.1 %qkv0.1 = (f32[16,128,128]{2,1,0:T(8,128)}, f32[4,128,128]{2,1,0:T(8,128)}, f32[4,128,128]{2,1,0:T(8,128)}, f32[128,128]{1,0:T(8,128)}, f32[128,128]{1,0:T(8,128)}, /*index=5*/bf16[128,4096]{1,0:T(8,128)(2,1)}) custom-call(s32[32]{0:T(128)} %len_ref.3, f32[512,128]{1,0:T(8,128)} %constant.2.clone.refs_1_, bf16[128,4096]{1,0:T(8,128)(2,1)} %bitcast.13, ...), custom_call_target="tpu_custom_call" | custom-call | tf_op jit(solution)/shard_map/qkv0/pallas_call | solution.py:111
  13.7 14.3 %attn0.1 = (bf16[2,32,1024,128]{3,2,1,0:T(8,128)(2,1)}, bf16[2,32,1024,128]{3,2,1,0:T(8,128)(2,1)}, f32[16,128,128]{2,1,0:T(8,128)}, f32[128,128]{1,0:T(8,128)}, f32[128,128]{1,0:T(8,128)}) custom-call(s32[32]{0:T(128)} %len_ref.3, f32[16,128,128]{2,1,0:T(8,128)} %get-tuple-element.23.q_ref, f32[4,128,128]{2,1,0:T(8,128)} %get-tuple-element.24.kn_ref, ...), custom_call_target="tpu_custom_call" | custom-call | tf_op jit(solution)/shard_map/attn0/pallas_call | solution.py:243
  28.0 80.4 %block0.1 = (bf16[128,4096]{1,0:T(8,128)(2,1)}, f32[16,128,128]{2,1,0:T(8,128)}, f32[4,128,128]{2,1,0:T(8,128)}, f32[4,128,128]{2,1,0:T(8,128)}) custom-call(f32[16,128,128]{2,1,0:T(8,128)} %get-tuple-element.26.o_hbm, f32[128,128]{1,0:T(8,128)} %get-tuple-element.27.sm_hbm, f32[128,128]{1,0:T(8,128)} %get-tuple-element.28.sl_hbm, ...), custom_call_target="tpu_custom_call" | custom-call | tf_op jit(solution)/shard_map/block0/pallas_call | solution.py:638
  108.4 14.2 %attn1.1 = (bf16[2,32,1024,128]{3,2,1,0:T(8,128)(2,1)}, bf16[2,32,1024,128]{3,2,1,0:T(8,128)(2,1)}, f32[16,128,128]{2,1,0:T(8,128)}, f32[128,128]{1,0:T(8,128)}, f32[128,128]{1,0:T(8,128)}) custom-call(s32[32]{0:T(128)} %len_ref.3, f32[16,128,128]{2,1,0:T(8,128)} %get-tuple-element.32.q_ref, ...), custom_call_target="tpu_custom_call", output_to_operand_aliasing={{0}: (6, {}), {1}: (7, {})} | custom-call | tf_op jit(solution)/shard_map/attn1/pallas_call | solution.py:243
  122.6 69.4 %block1.1 = bf16[128,4096]{1,0:T(8,128)(2,1)} custom-call(f32[16,128,128]{2,1,0:T(8,128)} %get-tuple-element.37.o_hbm, f32[128,128]{1,0:T(8,128)} %get-tuple-element.38.sm_hbm, f32[128,128]{1,0:T(8,128)} %get-tuple-element.39.sl_hbm, bf16[128,4096]{1,0:T(8,128)(2,1)} %get-tuple-element.40.u_hbm, bf16[2,4096]{1,0:T(2,128)(2,1)} %gain_ref.3, ...), custom_call_target="tpu_custom_call" | custom-call | tf_op jit(solution)/shard_map/block1/pallas_call | solution.py:638
  192.1 2.3 %copy.22 = bf16[4,32,4096]{2,1,0:T(8,128)(2,1)} copy(bf16[4,32,4096]{2,1,0:T(8,128)(2,1)} %bitcast.12) | data formatting | bytes 2097152

commit v5 on v4

--- a/solution.py
+++ b/solution.py
@@ -36,99 +36,70 @@
     return jnp.where(ci == src, 1.0, 0.0).astype(BF16)
 
 
-def qkv_kernel(layer, n_steps, first_pos, first, *refs):
-    if first:
-        len_ref, tab_ref, u_ref, gain_ref, wq_ref, wk_ref, wv_ref, q_ref, k_ref, v_ref, cos_ref, sin_ref, up_ref, h_scr = refs
-    else:
-        u_ref, gain_ref, cos_ref, sin_ref, wq_ref, wk_ref, wv_ref, q_ref, k_ref, v_ref, h_scr = refs
-    rows, d_model = u_ref.shape
-    hd = cos_ref.shape[1]
-
-    @pl.when(pl.program_id(0) == 0)
-    def _():
-        x = u_ref[...].astype(F32)
-        inv = lax.rsqrt(jnp.sum(x * x, axis=-1, keepdims=True) * (1.0 / d_model) + EPS)
-        h = (x * inv * gain_ref[layer:layer + 1, :].astype(F32)).astype(BF16)
-        if first:
-            perm = permutation(rows, n_steps, True)
-            h_scr[...] = jnp.dot(perm, h, preferred_element_type=F32).astype(BF16)
-            up_ref[...] = jnp.dot(perm, u_ref[...], preferred_element_type=F32).astype(BF16)
-            for b in range(rows // n_steps):
-                cos_ref[b * n_steps:(b + 1) * n_steps, :] = tab_ref[pl.ds(len_ref[b] - first_pos, n_steps), :]
-            both = cos_ref[...]
-            swap = pltpu.roll(both, hd // 2, 1)
-            low = lax.broadcasted_iota(jnp.int32, both.shape, 1) < hd // 2
-            cos_ref[...] = jnp.where(low, both, swap)
-            sin_ref[...] = jnp.where(low, -swap, both)
-        else:
-            h_scr[...] = h
-
-    h = h_scr[...]
-    cos_a, sin_a = cos_ref[...], sin_ref[...]
-
-    def rot(x):
-        return (x * cos_a + pltpu.roll(x, hd // 2, 1) * sin_a).astype(BF16).astype(F32)
-
-    q = jnp.dot(h, wq_ref[0], preferred_element_type=F32)
-    for j in range(q_ref.shape[0]):
-        q_ref[j] = rot(q[:, j * hd:(j + 1) * hd])
-    k = jnp.dot(h, wk_ref[0], preferred_element_type=F32)
-    k_ref[0] = rot(k)
-    v = jnp.dot(h, wv_ref[0], preferred_element_type=F32)
-    v_ref[0] = v.astype(BF16).astype(F32)
-
-
-def qkv_call(layer, u, gain, rope, lengths, wq, wk, wv, n_steps, hd, first_pos):
-    rows, d_model = u.shape
-    kv_loc = wk.shape[2] // hd
-    heads = wq.shape[2] // hd
-    grp = heads // kv_loc
-    first = layer == 0
-    full = lambda shape: pl.BlockSpec(shape, lambda j: (0,) * len(shape))
-    weights = [
-        pl.BlockSpec((1, d_model, grp * hd), lambda j: (layer, 0, j)),
-        pl.BlockSpec((1, d_model, hd), lambda j: (layer, 0, j)),
-        pl.BlockSpec((1, d_model, hd), lambda j: (layer, 0, j)),
-    ]
-    out_specs = [
-        pl.BlockSpec((grp, rows, hd), lambda j: (j, 0, 0)),
-        pl.BlockSpec((1, rows, hd), lambda j: (j, 0, 0)),
-        pl.BlockSpec((1, rows, hd), lambda j: (j, 0, 0)),
-    ]
-    out_shape = [
-        jax.ShapeDtypeStruct((heads, rows, hd), F32),
-        jax.ShapeDtypeStruct((kv_loc, rows, hd), F32),
-        jax.ShapeDtypeStruct((kv_loc, rows, hd), F32),
-    ]
-    if first:
-        args = [lengths, rope, u, gain, wq, wk, wv]
-        in_specs = [pl.BlockSpec(memory_space=pltpu.SMEM), full(rope.shape), full(u.shape), full(gain.shape)] + weights
-        out_specs += [full((rows, hd)), full((rows, hd)), full((rows, d_model))]
-        out_shape += [jax.ShapeDtypeStruct((rows, hd), F32)] * 2 + [jax.ShapeDtypeStruct((rows, d_model), BF16)]
-    else:
-        args = [u, gain, *rope, wq, wk, wv]
-        in_specs = [full(u.shape), full(gain.shape), full((rows, hd)), full((rows, hd))] + weights
-    return pl.pallas_call(
-        functools.partial(qkv_kernel, layer, n_steps, first_pos, first),
-        grid=(kv_loc,),
-        in_specs=in_specs,
-        out_specs=out_specs,
-        out_shape=out_shape,
-        scratch_shapes=[pltpu.VMEM((rows, d_model), BF16)],
-        compiler_params=pltpu.CompilerParams(vmem_limit_bytes=VMEM_ALL),
-        name=f'qkv{layer}',
-    )(*args)
-
-
 SEQS = 4
 SLOTS = 8
 AHEAD = 8
 
 
-def attn_kernel(layer, n_kv, n_steps, sp_size, has_prev, len_ref, q_ref, kn_ref, vn_ref, k_hbm, v_hbm, *rest):
-    if has_prev:
-        rest = rest[2:]
+def attn_kernel(layer, n_kv, n_steps, sp_size, len_ref, q_ref, kn_ref, vn_ref, k_hbm, v_hbm, _k, _v, *rest):
     ko_hbm, vo_hbm, o_ref, sm_ref, sl_ref, code, kb, vb, in_sem, out_sem = rest
+    attn_body(layer, n_kv, n_steps, sp_size, lambda: None, len_ref, q_ref, kn_ref, vn_ref, k_hbm, v_hbm,
+              ko_hbm, vo_hbm, o_ref, sm_ref, sl_ref, code, kb, vb, in_sem, out_sem)
+
+
+def first_kernel(n_kv, n_steps, sp_size, first_pos, len_ref, tab_ref, u_ref, gain_ref, wq_hbm, wk_hbm, wv_hbm, k_hbm, v_hbm,
+                 ko_hbm, vo_hbm, o_ref, sm_ref, sl_ref, cos_ref, sin_ref, up_ref,
+                 q_s, k_s, v_s, h_scr, wq_v, wk_v, wv_v, w_sem, code, kb, vb, in_sem, out_sem):
+    rows, d_model = u_ref.shape
+    hd = cos_ref.shape[1]
+    n_q, _, cols = wq_v.shape
+    fetch = [pltpu.make_async_copy(wq_hbm.at[0, :, j * cols:(j + 1) * cols], wq_v.at[j], w_sem.at[j]) for j in range(n_q)]
+    fetch.append(pltpu.make_async_copy(wk_hbm.at[0], wk_v, w_sem.at[n_q]))
+    fetch.append(pltpu.make_async_copy(wv_hbm.at[0], wv_v, w_sem.at[n_q + 1]))
+    for cp in fetch:
+        cp.start()
+
+    def qkv():
+        x = u_ref[...].astype(F32)
+        inv = lax.rsqrt(jnp.sum(x * x, axis=-1, keepdims=True) * (1.0 / d_model) + EPS)
+        h = (x * inv * gain_ref[0:1, :].astype(F32)).astype(BF16)
+        perm = permutation(rows, n_steps, True)
+        h_scr[...] = jnp.dot(perm, h, preferred_element_type=F32).astype(BF16)
+        up_ref[...] = jnp.dot(perm, u_ref[...], preferred_element_type=F32).astype(BF16)
+        for b in range(rows // n_steps):
+            cos_ref[b * n_steps:(b + 1) * n_steps, :] = tab_ref[pl.ds(len_ref[b] - first_pos, n_steps), :]
+        both = cos_ref[...]
+        swap = pltpu.roll(both, hd // 2, 1)
+        low = lax.broadcasted_iota(jnp.int32, both.shape, 1) < hd // 2
+        cos_a = jnp.where(low, both, swap)
+        sin_a = jnp.where(low, -swap, both)
+        cos_ref[...] = cos_a
+        sin_ref[...] = sin_a
+
+        def rot(z):
+            return (z * cos_a + pltpu.roll(z, hd // 2, 1) * sin_a).astype(BF16).astype(F32)
+
+        per = cols // hd
+        for j in range(n_q):
+            fetch[j].wait()
+            q = jnp.dot(h_scr[...], wq_v[j], preferred_element_type=F32)
+            for e in range(per):
+                q_s[j * per + e] = rot(q[:, e * hd:(e + 1) * hd])
+        fetch[n_q].wait()
+        k = jnp.dot(h_scr[...], wk_v[...], preferred_element_type=F32)
+        for e in range(n_kv):
+            k_s[e] = rot(k[:, e * hd:(e + 1) * hd])
+        fetch[n_q + 1].wait()
+        v = jnp.dot(h_scr[...], wv_v[...], preferred_element_type=F32)
+        for e in range(n_kv):
+            v_s[e] = v[:, e * hd:(e + 1) * hd].astype(BF16).astype(F32)
+
+    attn_body(0, n_kv, n_steps, sp_size, qkv, len_ref, q_s, k_s, v_s, k_hbm, v_hbm,
+              ko_hbm, vo_hbm, o_ref, sm_ref, sl_ref, code, kb, vb, in_sem, out_sem)
+
+
+def attn_body(layer, n_kv, n_steps, sp_size, ahead, len_ref, q_ref, kn_ref, vn_ref, k_hbm, v_hbm,
+              ko_hbm, vo_hbm, o_ref, sm_ref, sl_ref, code, kb, vb, in_sem, out_sem):
     my_sp = lax.axis_index('sp').astype(jnp.int32)
     heads, all_rows, hd = q_ref.shape
     n_batch = all_rows // n_steps
@@ -165,6 +136,7 @@
     row16 = lax.broadcasted_iota(jnp.int32, (16, hd), 0)
     lane = lax.broadcasted_iota(jnp.int32, sm_ref.shape, 1)
     per = 16 // n_kv
+    ahead()
 
     def body(i, _):
         slot_b = lax.rem(i, SLOTS)
@@ -227,32 +199,50 @@
             cp.wait()
 
 
-def attn_call(layer, lengths, q, kn, vn, kc, vc, prev, n_kv, n_steps, sp_size):
+def attn_call(layer, lengths, ins, kc, vc, prev, n_kv, n_steps, sp_size, first_pos):
     n_layers, n_batch, n_cols, hd = kc.shape
-    heads, rows, _ = q.shape
+    rows = n_batch * n_steps
+    V = pltpu.VMEM
+    dma = pltpu.SemaphoreType.DMA
+    vm = pl.BlockSpec(memory_space=V)
+    hbm = pl.BlockSpec(memory_space=pl.ANY)
+    smem = pl.BlockSpec(memory_space=pltpu.SMEM)
+    if prev is None:
+        table, u, gain, wq, wk, wv = ins
+        heads, d_model = wq.shape[2] // hd, u.shape[1]
+        cols = wk.shape[2]
+        kernel = functools.partial(first_kernel, n_kv, n_steps, sp_size, first_pos)
+        in_specs = [smem, vm, vm, vm, hbm, hbm, hbm, hbm, hbm]
+        args = [lengths, *ins, kc, vc]
+        aliases = {}
+        more_out = [jax.ShapeDtypeStruct((rows, hd), F32)] * 2 + [jax.ShapeDtypeStruct(u.shape, BF16)]
+        scratch = [
+            V((heads, rows, hd), F32), V((n_kv, rows, hd), F32), V((n_kv, rows, hd), F32), V(u.shape, BF16),
+            V((wq.shape[2] // cols, d_model, cols), BF16), V((d_model, cols), BF16), V((d_model, cols), BF16),
+            dma((wq.shape[2] // cols + 2,)),
+        ]
+    else:
+        heads = ins[0].shape[0]
+        kernel = functools.partial(attn_kernel, layer, n_kv, n_steps, sp_size)
+        in_specs = [smem, vm, vm, vm, hbm, hbm, hbm, hbm]
+        args = [lengths, *ins, kc, vc, *prev]
+        aliases = {6: 0, 7: 1}
+        more_out = []
+        scratch = []
     srows = heads * 2 * n_steps
-    vm = pl.BlockSpec(memory_space=pltpu.VMEM)
-    hbm = pl.BlockSpec(memory_space=pl.ANY)
-    in_specs = [pl.BlockSpec(memory_space=pltpu.SMEM), vm, vm, vm, hbm, hbm]
-    args = [lengths, q, kn, vn, kc, vc]
-    aliases = {}
-    if prev is not None:
-        in_specs += [hbm, hbm]
-        args += list(prev)
-        aliases = {6: 0, 7: 1}
     return pl.pallas_call(
-        functools.partial(attn_kernel, layer, n_kv, n_steps, sp_size, prev is not None),
+        kernel,
         in_specs=in_specs,
-        out_specs=[hbm, hbm, vm, vm, vm],
+        out_specs=[hbm, hbm, vm, vm, vm] + [vm] * len(more_out),
         out_shape=[
             jax.ShapeDtypeStruct(kc.shape, kc.dtype), jax.ShapeDtypeStruct(vc.shape, vc.dtype),
             jax.ShapeDtypeStruct((heads, rows, hd), F32),
             jax.ShapeDtypeStruct((srows, 128), F32), jax.ShapeDtypeStruct((srows, 128), F32),
-        ],
-        scratch_shapes=[
-            pltpu.VMEM((srows, n_cols), jnp.int32),
-            pltpu.VMEM((SLOTS, SEQS, n_cols, hd), BF16), pltpu.VMEM((SLOTS, SEQS, n_cols, hd), BF16),
-            pltpu.SemaphoreType.DMA((SLOTS, 2)), pltpu.SemaphoreType.DMA((SLOTS, 2)),
+        ] + more_out,
+        scratch_shapes=scratch + [
+            V((srows, n_cols), jnp.int32),
+            V((SLOTS, SEQS, n_cols, hd), BF16), V((SLOTS, SEQS, n_cols, hd), BF16),
+            dma((SLOTS, 2)), dma((SLOTS, 2)),
         ],
         input_output_aliases=aliases,
         compiler_params=pltpu.CompilerParams(vmem_limit_bytes=VMEM_ALL),
@@ -675,9 +665,10 @@
         prev = None
         for layer in range(n_layers):
             last = layer == n_layers - 1
+            ins = (table, u, gain_attn, w_query, w_key, w_value) if layer == 0 else (q, k, v)
+            nk, nv, o, sm, sl, *more = attn_call(layer, lengths, ins, kc, vc, prev, kv_loc, n_steps, sp_size, first_pos)
             if layer == 0:
-                q, k, v, cos_a, sin_a, u = qkv_call(layer, u, gain_attn, table, lengths, w_query, w_key, w_value, n_steps, hd, first_pos)
-            nk, nv, o, sm, sl = attn_call(layer, lengths, q, k, v, kc, vc, prev, kv_loc, n_steps, sp_size)
+                cos_a, sin_a, u = more
             prev = (nk, nv)
             nxt = () if last else (gain_attn, cos_a, sin_a, w_query, w_key, w_value)
             outs = block_call(layer, last, n_steps, o, sm, sl, u, gain_mlp, w_out, w_gate, w_up, w_down, sp_size, nxt)

time: 195 us -> 194 us (level)
    pallas_call x3 -> x2, Pallas kernels: 41.6 us -> 41.3 us  [attn_call(): pl.pallas_call(kernel, in_specs=in_specs, out_specs=[hbm, hbm, vm, vm, vm...]
where the time goes in v5:
time: 194 us
  Pallas kernels  191 us (98%)
  local copies, waits for them, and re-layouts  2.29 us (1%)
    pallas_call x2, Pallas kernels, block_call(): pl.pallas_call(functools.partial(block_kernel, layer, last, n_steps), out...  149 us
    pallas_call x2, Pallas kernels, attn_call(): pl.pallas_call(kernel, in_specs=in_specs, out_specs=[hbm, hbm, vm, vm, vm...  41.3 us

profile of v5, /device:TPU:0, one launch (start us, length us, event | category | flops | bytes accessed | tf_op | source)
XLA Modules:
  0.0 193.6 jit_solution(12081915401515133167)
XLA Ops:
  0.6 27.1 %attn0.1 = (bf16[2,32,1024,128]{3,2,1,0:T(8,128)(2,1)}, bf16[2,32,1024,128]{3,2,1,0:T(8,128)(2,1)}, f32[16,128,128]{2,1,0:T(8,128)}, f32[128,128]{1,0:T(8,128)},...) custom-call(s32[32]{0:T(128)} %len_ref.3, ...), custom_call_target="tpu_custom_call" | custom-call | tf_op jit(solution)/shard_map/attn0/pallas_call | solution.py:233
  27.7 80.3 %block0.1 = (bf16[128,4096]{1,0:T(8,128)(2,1)}, f32[16,128,128]{2,1,0:T(8,128)}, f32[4,128,128]{2,1,0:T(8,128)}, f32[4,128,128]{2,1,0:T(8,128)}) custom-call(f32[16,128,128]{2,1,0:T(8,128)} %get-tuple-element.20.o_hbm, f32[128,128]{1,0:T(8,128)} %get-tuple-element.21.sm_hbm, f32[128,128]{1,0:T(8,128)} %get-tuple-element.22.sl_hbm, ...), custom_call_target="tpu_custom_call" | custom-call | tf_op jit(solution)/shard_map/block0/pallas_call | solution.py:628
  108.0 14.2 %attn1.1 = (bf16[2,32,1024,128]{3,2,1,0:T(8,128)(2,1)}, bf16[2,32,1024,128]{3,2,1,0:T(8,128)(2,1)}, f32[16,128,128]{2,1,0:T(8,128)}, f32[128,128]{1,0:T(8,128)}, f32[128,128]{1,0:T(8,128)}) custom-call(s32[32]{0:T(128)} %len_ref.3, f32[16,128,128]{2,1,0:T(8,128)} %get-tuple-element.26.q_ref, ...), custom_call_target="tpu_custom_call", output_to_operand_aliasing={{0}: (6, {}), {1}: (7, {})} | custom-call | tf_op jit(solution)/shard_map/attn1/pallas_call | solution.py:233
  122.2 69.1 %block1.1 = bf16[128,4096]{1,0:T(8,128)(2,1)} custom-call(f32[16,128,128]{2,1,0:T(8,128)} %get-tuple-element.31.o_hbm, f32[128,128]{1,0:T(8,128)} %get-tuple-element.32.sm_hbm, f32[128,128]{1,0:T(8,128)} %get-tuple-element.33.sl_hbm, bf16[128,4096]{1,0:T(8,128)(2,1)} %get-tuple-element.34.u_hbm, bf16[2,4096]{1,0:T(2,128)(2,1)} %gain_ref.5, ...), custom_call_target="tpu_custom_call" | custom-call | tf_op jit(solution)/shard_map/block1/pallas_call | solution.py:628
  191.3 2.3 %copy.22 = bf16[4,32,4096]{2,1,0:T(8,128)(2,1)} copy(bf16[4,32,4096]{2,1,0:T(8,128)(2,1)} %bitcast.12) | data formatting | bytes 2097152
